TPU v7x, 32 devices: a whole 2x2x4 slice. The times are simulated.
32 devices in a mesh: row: 4 (over z), col: 8 (over y, x, core).
Axes of the slice: x: 2, y: 2, z: 4, core: 2. Of those that a mesh axis runs over, the one named last changes fastest.
Arguments:
- tokens: bfloat16 [2048, 2048], P(('row', 'col')), may hold values from -6 to 6
- timestep: int32 [1], replicated, may hold values from 0 to 999
- mod_weight: float32 [256, 2048], replicated, may hold values from -0.375 to 0.375
- qkv_weight: bfloat16 [3, 2048, 2048], P(None, None, 'col'), may hold values from -0.125 to 0.125
- attn_scale: float32 [16], P('col'), may hold values from 4 to 40
- out_weight: bfloat16 [2048, 2048], P('col'), may hold values from -0.5 to 0.5
- grad_update: bfloat16 [2048, 2048], P(('row', 'col')), may hold values from -6 to 6
Outputs:
- update: bfloat16 [2048, 2048], P(('row', 'col'))
- grad_tokens: bfloat16 [2048, 2048], P(('row', 'col'))
- grad_qkv: float32 [3, 2048, 2048], P(None, 'row', 'col')
- grad_out: float32 [2048, 2048], P('col', 'row')
All inputs are finite; a program needn't handle non-finite values.
Results may differ from a plain program's by a relative error of at most 0.018.
Values may be sent and summed in bfloat16 or wider, within the bound.
A program may use at most 128 MiB of HBM per device.

v0:
```python
import functools
import math

import jax
import jax.numpy as jnp
from jax import lax
from jax.experimental import pallas as pl
from jax.experimental.pallas import tpu as pltpu
from jax.sharding import PartitionSpec as P

epsilon = 1e-06
MESH = pl.DeviceIdType.MESH
RELAYED = 4


def embed(timestep, count):
    index = jnp.arange(count, dtype=jnp.float32)
    freqs = jnp.exp(-math.log(10000.0) * index / count)
    angles = timestep.astype(jnp.float32)[0] * freqs
    return jnp.concatenate([jnp.cos(angles), jnp.sin(angles)])


def by_head(array, head_dim):
    return [array[:, at : at + head_dim] for at in range(0, array.shape[1], head_dim)]


def unit_rows(values):
    factor = lax.rsqrt(jnp.mean(values * values, -1, keepdims=True) + epsilon)
    return (values * factor, factor)


def unit_grad(grad_unit, unit, factor):
    return factor * (grad_unit - unit * jnp.mean(grad_unit * unit, -1, keepdims=True))


def piece(ref, dim, size, index):
    start = index * size
    if isinstance(start, int):
        pass
    elif dim == len(ref.shape) - 1:
        start = pl.multiple_of(start, 128)
    elif dim == len(ref.shape) - 2:
        start = pl.multiple_of(start, 16)
    return ref.at[(slice(None),) * dim + (pl.ds(start, size),)]


def half(ref, side):
    dim = len(ref.shape) - 2
    size = ref.shape[dim] // 2
    return ref.at[(slice(None),) * dim + (pl.ds(side * size, size),)]


def exchange_kernel(plan, *refs):
    count = len(plan)
    sources, targets = refs[:count], refs[count : 2 * count]
    own_sem, send_sem, recv_sem = refs[2 * count : 2 * count + 3]
    relays = refs[2 * count + 3 :]
    sizes = {axis: n for axis, n, dim, size in plan}
    barrier = pltpu.get_barrier_semaphore()
    for axis, n in sizes.items():
        me = lax.axis_index(axis)
        for step in range(1, n):
            pl.semaphore_signal(
                barrier, inc=1, device_id={axis: lax.rem(me + step, n)}, device_id_type=MESH
            )
    pl.semaphore_wait(barrier, sum(n - 1 for n in sizes.values()))
    def send(job, slot, source, target, peer):
        copy = pltpu.make_async_remote_copy(
            src_ref=source,
            dst_ref=target,
            send_sem=send_sem.at[job, slot],
            recv_sem=recv_sem.at[job, slot],
            device_id={plan[job][0]: peer},
            device_id_type=MESH,
        )
        copy.start()
        return copy

    copies, hops = [], {}
    chained = [job for job in range(count) if plan[job][1] == RELAYED and plan[job][2] is not None]
    relayed = [job for job in range(count) if plan[job][1] == RELAYED and job not in chained]
    for step in range(1, max(sizes.values())):
        for job, (axis, n, dim, size) in enumerate(plan):
            if step >= n or job in chained or (n == RELAYED and step == 2):
                continue
            me = lax.axis_index(axis)
            peer = lax.rem(me + step, n)
            source = sources[job]
            source = source if dim is None else piece(source, dim, size, peer)
            copy = send(job, step, source, targets[job].at[me], peer)
            if n == RELAYED and dim is None:
                hops.setdefault(job, []).append(copy)
            else:
                copies.append(copy)
    for job, (axis, n, dim, size) in enumerate(plan):
        if job in chained:
            continue
        me = lax.axis_index(axis)
        source = sources[job]
        copy = pltpu.make_async_copy(
            source if dim is None else piece(source, dim, size, me),
            targets[job].at[me],
            own_sem.at[job],
        )
        copy.start()
        copies.append(copy)
    for side in range(2):
        for job in relayed:
            axis, n, dim, size = plan[job]
            me = lax.axis_index(axis)
            right, left = lax.rem(me + 1, n), lax.rem(me + 3, n)
            onward, origin = (right, left) if side == 0 else (left, right)
            hops[job][side].wait_recv()
            landing = half(targets[job].at[origin], side)
            copies.append(send(job, 6 + side, landing, landing, onward))
    def link(job, way, owner, source):
        axis = plan[job][0]
        me = lax.axis_index(axis)
        slot = owner - 1 if way == 0 else owner
        return pltpu.make_async_remote_copy(
            src_ref=relays[job].at[way, slot] if source is None else source,
            dst_ref=relays[job].at[way, slot],
            send_sem=send_sem.at[job, 3 * way + slot],
            recv_sem=recv_sem.at[job, 3 * way + slot],
            device_id={axis: lax.rem(me + (1 if way == 0 else RELAYED - 1), RELAYED)},
            device_id_type=MESH,
        )

    def forward(job, way, owner, place):
        axis, n, dim, size = plan[job]
        mine = piece(sources[job], dim, size, owner)

        @pl.when(lax.axis_index(axis) == place)
        def _():
            if place == (0 if way == 0 else n - 1):
                link(job, way, owner, mine).start()
            else:
                copy = link(job, way, owner, None)
                copy.wait_recv()
                inbox = relays[job].at[way, owner - 1 if way == 0 else owner]
                total = inbox[...].astype(jnp.float32) + mine[...].astype(jnp.float32)
                inbox[...] = total.astype(inbox.dtype)
                copy.start()

    order = [(0, 3, 0), (1, 0, 3), (0, 2, 0), (1, 1, 3), (0, 1, 0), (1, 2, 3)]
    order += [(0, 3, 1), (1, 0, 2), (0, 2, 1), (1, 1, 2), (0, 3, 2), (1, 0, 1)]
    for way, owner, place in order:
        for job in chained:
            forward(job, way, owner, place)
    for job in chained:
        axis, n, dim, size = plan[job]
        for owner in range(n):

            @pl.when(lax.axis_index(axis) == owner)
            def _():
                total = piece(sources[job], dim, size, owner)[...].astype(jnp.float32)
                if owner > 0:
                    link(job, 0, owner, None).wait_recv()
                    total = total + relays[job][0, owner - 1].astype(jnp.float32)
                if owner < n - 1:
                    link(job, 1, owner, None).wait_recv()
                    total = total + relays[job][1, owner].astype(jnp.float32)
                targets[job][0] = total
                for other in range(n):
                    if other > owner:
                        link(job, 0, other, None).wait_send()
                    if other < owner:
                        link(job, 1, other, None).wait_send()

    for job in relayed:
        for copy in hops[job]:
            copy.wait_send()
    for copy in copies:
        copy.wait()


def exchange(jobs, collective_id):
    plan, shapes, relays = [], [], []
    for array, axis, dim in jobs:
        n = lax.axis_size(axis)
        block = list(array.shape)
        size = None
        if dim is not None:
            size = block[dim] = block[dim] // n
        plan.append((axis, n, dim, size))
        if n == RELAYED and dim is not None:
            shapes.append(jax.ShapeDtypeStruct((1,) + tuple(block), jnp.float32))
            relays.append(pltpu.VMEM((2, n - 1) + tuple(block), array.dtype))
        else:
            shapes.append(jax.ShapeDtypeStruct((n,) + tuple(block), array.dtype))
            relays.append(pltpu.VMEM((16, 128), array.dtype))
    most = max(2 * RELAYED, max(n for axis, n, dim, size in plan))
    count = len(jobs)
    in_vmem = pl.BlockSpec(memory_space=pltpu.VMEM)
    return pl.pallas_call(
        functools.partial(exchange_kernel, tuple(plan)),
        out_shape=shapes,
        in_specs=[in_vmem] * count,
        out_specs=[in_vmem] * count,
        scratch_shapes=[
            pltpu.SemaphoreType.DMA((count,)),
            pltpu.SemaphoreType.DMA((count, most)),
            pltpu.SemaphoreType.DMA((count, most)),
            *relays,
        ],
        compiler_params=pltpu.CompilerParams(
            collective_id=collective_id, has_side_effects=True, vmem_limit_bytes=48 * 2**20
        ),
        name=f"exchange_{collective_id}",
    )(*[array for array, axis, dim in jobs])


def dot_rows(left, right):
    return lax.dot_general(
        left, right, (((1,), (1,)), ((), ())), preferred_element_type=jnp.float32
    )


def dot_columns(left, right):
    return lax.dot_general(
        left, right, (((0,), (0,)), ((), ())), preferred_element_type=jnp.float32
    )


def attention_kernel(
    scale_ref, q_ref, k_ref, v_ref, g_ref, o_ref, dq_ref, dk_ref, dv_ref, dk_sum, dv_sum
):
    block = pl.program_id(1)
    scale = scale_ref[pl.program_id(0)]
    coeff = scale * (1.0 / q_ref.shape[1])
    query, keys, values, grad = q_ref[...], k_ref[...], v_ref[...], g_ref[...]
    weights = jnp.exp(dot_rows(query, keys) * coeff - scale)
    inverse = 1.0 / jnp.sum(weights, -1, keepdims=True)
    mixed = jnp.dot(weights.astype(jnp.bfloat16), values, preferred_element_type=jnp.float32)
    attended = (mixed * inverse).astype(jnp.bfloat16)
    o_ref[...] = attended
    delta = jnp.sum(
        grad.astype(jnp.float32) * attended.astype(jnp.float32), -1, keepdims=True
    )
    probs = weights * inverse
    dscores = (probs * (dot_rows(grad, values) - delta) * coeff).astype(jnp.bfloat16)
    dq_ref[...] = jnp.dot(dscores, keys, preferred_element_type=jnp.float32)
    dk_part = dot_columns(dscores, query)
    dv_part = dot_columns(probs.astype(jnp.bfloat16), grad)

    @pl.when(block == 0)
    def _():
        dk_sum[...] = dk_part
        dv_sum[...] = dv_part

    @pl.when(block > 0)
    def _():
        dk_sum[...] += dk_part
        dv_sum[...] += dv_part

    @pl.when(block == pl.num_programs(1) - 1)
    def _():
        dk_ref[...] = dk_sum[...].astype(jnp.bfloat16)
        dv_ref[...] = dv_sum[...].astype(jnp.bfloat16)


def attention(attn_scale, queries, keys_values, grads):
    heads = attn_scale.shape[0]
    span, inner = queries.shape
    length = keys_values.shape[0]
    head_dim = inner // heads
    size = math.gcd(span, 256)
    while size * length > 2**19 and size % 32 == 0:
        size //= 2
    mine = pl.BlockSpec((size, head_dim), lambda h, i: (i, h))
    keys = pl.BlockSpec((length, head_dim), lambda h, i: (0, h))
    values = pl.BlockSpec((length, head_dim), lambda h, i: (0, heads + h))
    return pl.pallas_call(
        attention_kernel,
        grid=(heads, span // size),
        out_shape=[
            jax.ShapeDtypeStruct((span, inner), jnp.bfloat16),
            jax.ShapeDtypeStruct((span, inner), jnp.float32),
            jax.ShapeDtypeStruct((length, inner), jnp.bfloat16),
            jax.ShapeDtypeStruct((length, inner), jnp.bfloat16),
        ],
        in_specs=[pl.BlockSpec(memory_space=pltpu.SMEM), mine, keys, values, mine],
        out_specs=[mine, mine, keys, keys],
        scratch_shapes=[pltpu.VMEM((length, head_dim), jnp.float32)] * 2,
        compiler_params=pltpu.CompilerParams(
            dimension_semantics=("arbitrary", "arbitrary"), vmem_limit_bytes=56 * 2**20
        ),
        name="attention",
    )(attn_scale, queries, keys_values, keys_values, grads)


def add_up(slots):
    return jnp.sum(slots.astype(jnp.float32), 0)


def per_device(tokens, timestep, mod_weight, qkv_weight, attn_scale, out_weight, grad_update):
    tok_dev, width = tokens.shape
    heads_here = attn_scale.shape[0]
    inner = qkv_weight.shape[2]
    head_dim = inner // heads_here
    span = tok_dev * lax.axis_size("col")
    embedded = embed(timestep, mod_weight.shape[0] // 2)
    gain = 1.0 + jnp.sum(embedded[:, None] * mod_weight, 0)
    tok_float = tokens.astype(jnp.float32)
    rstd = lax.rsqrt(jnp.mean(tok_float * tok_float, -1, keepdims=True) + epsilon)
    normed = tok_float * rstd
    hidden = (normed * gain).astype(jnp.bfloat16)
    (group,) = exchange([(hidden, "col", None)], 0)
    group = group.reshape(span, width)
    raw = [jnp.dot(group, qkv_weight[k], preferred_element_type=jnp.float32) for k in range(3)]
    query_unit, query_factor = zip(*[unit_rows(part) for part in by_head(raw[0], head_dim)])
    key_unit, key_factor = zip(*[unit_rows(part) for part in by_head(raw[1], head_dim)])
    queries = jnp.concatenate(query_unit, 1).astype(jnp.bfloat16)
    keys_values = jnp.concatenate(key_unit + (raw[2],), 1).astype(jnp.bfloat16)
    all_keys_values, grad_group = exchange(
        [(keys_values, "row", None), (grad_update, "col", None)], 1
    )
    all_keys_values = all_keys_values.reshape(-1, 2 * inner)
    grad_group = grad_group.reshape(span, width)
    grad_attended = dot_rows(grad_group, out_weight).astype(jnp.bfloat16)
    attended, grad_query, key_part, value_part = attention(
        attn_scale, queries, all_keys_values, grad_attended
    )
    update_part = jnp.dot(attended, out_weight, preferred_element_type=jnp.float32).astype(
        jnp.bfloat16
    )
    out_part = dot_columns(attended, grad_group).astype(jnp.bfloat16)
    key_slots, value_slots, update_slots = exchange(
        [(key_part, "row", 0), (value_part, "row", 0), (update_part, "col", 0)], 2
    )
    update = add_up(update_slots).astype(jnp.bfloat16)

    def raw_grads(grad_unit, unit, factor):
        parts = zip(by_head(grad_unit, head_dim), unit, factor)
        return jnp.concatenate([unit_grad(*part) for part in parts], 1).astype(jnp.bfloat16)

    grad_raw = [
        raw_grads(grad_query, query_unit, query_factor),
        raw_grads(add_up(key_slots), key_unit, key_factor),
        add_up(value_slots).astype(jnp.bfloat16),
    ]
    qkv_part = jnp.stack([dot_columns(group, part).astype(jnp.bfloat16) for part in grad_raw])
    hidden_part = (
        sum(dot_rows(part, qkv_weight[k]) for k, part in enumerate(grad_raw))
    ).astype(jnp.bfloat16)
    qkv_slots, hidden_slots, out_slots = exchange(
        [(qkv_part, "row", 1), (hidden_part, "col", 0), (out_part, "row", 1)], 3
    )
    grad_qkv = add_up(qkv_slots)
    grad_out = add_up(out_slots)
    grad_normed = add_up(hidden_slots) * gain
    grad_tokens = (
        rstd * (grad_normed - normed * jnp.mean(grad_normed * normed, -1, keepdims=True))
    ).astype(jnp.bfloat16)
    return (update, grad_tokens, grad_qkv, grad_out)


def solution(mesh):
    placed = (
        P(("row", "col"), None),
        P(),
        P(),
        P(None, None, "col"),
        P("col"),
        P("col", None),
        P(("row", "col"), None),
    )
    return jax.shard_map(
        per_device,
        mesh=mesh,
        in_specs=placed,
        out_specs=(
            P(("row", "col"), None),
            P(("row", "col"), None),
            P(None, "row", "col"),
            P("col", "row"),
        ),
        check_vma=False,
    )
```

profile of v0, /device:TPU:0, one launch (start us, length us, event | category | flops | bytes accessed | tf_op | source)
XLA Modules:
  0.0 233.7 jit_solution(14060379106294128959)
XLA Ops:
  1.4 1.1 fusion.27
  2.6 2.0 multiply_reduce_fusion
  4.7 27.1 %exchange_0.1 = bf16[8,64,2048]{2,1,0:T(8,128)(2,1)S(1)} custom-call(bf16[64,2048]{1,0:T(8,128)(2,1)S(1)} %fusion.22.refs_0_), custom_call_target="tpu_custom_call" | custom-call | tf_op jit(solution)/shard_map/exchange_0/pallas_call | solution.py:195
  31.9 0.7 convolution_convert_fusion.6
  32.6 0.7 fusion.7
  33.8 0.7 fusion.11
  35.0 0.7 pad_maximum_fusion.2.q_ref
  35.7 41.1 %exchange_1.1 = (bf16[4,512,512]{2,1,0:T(8,128)(2,1)S(1)}, bf16[8,64,2048]{2,1,0:T(8,128)(2,1)S(1)}) custom-call(bf16[512,512]{1,0:T(8,128)(2,1)S(1)} %pad_maximum_fusion.1.refs_0_, bf16[64,2048]{1,0:T(8,128)(2,1)S(1)} %copy-done.7), custom_call_target="tpu_custom_call" | custom-call | tf_op jit(solution)/shard_map/exchange_1/pallas_call | solution.py:195
  76.8 1.3 copy-done.1
  78.1 1.5 convolution_convert_fusion.5.g_ref
  79.6 11.7 %attention.1 = (bf16[512,256]{1,0:T(8,128)(2,1)}, f32[512,256]{1,0:T(8,128)}, bf16[2048,256]{1,0:T(8,128)(2,1)}, bf16[2048,256]{1,0:T(8,128)(2,1)}) custom-call(f32[2]{0:T(128)} %scale_ref.1, bf16[512,256]{1,0:T(8,128)(2,1)} %pad_maximum_fusion.2.q_ref, bf16[2048,512]{1,0:T(8,128)(2,1)} %bitcast.45, bf16[2048,512]{1,0:T(8,128)(2,1)} %bitcast.46, ...), custom_call_target="tpu_custom_call" | custom-call | tf_op jit(solution)/shard_map/attention/pallas_call | solution.py:273
  91.3 1.7 convolution_convert_fusion.1.refs_2_
  93.0 0.4 multiply_reduce_fusion.4
  93.8 1.7 fusion
  95.6 2.0 convolution_convert_fusion.refs_2_
  97.6 40.7 %exchange_2.1 = (f32[1,512,256]{2,1,0:T(8,128)S(1)}, f32[1,512,256]{2,1,0:T(8,128)S(1)}, bf16[8,64,2048]{2,1,0:T(8,128)(2,1)S(1)}) custom-call(bf16[2048,256]{1,0:T(8,128)(2,1)S(1)} %copy-done.5, bf16[2048,256]{1,0:T(8,128)(2,1)S(1)} %copy-done.6, bf16[512,2048]{1,0:T(8,128)(2,1)} %convolution_convert_fusion.refs_2_), custom_call_target="tpu_custom_call" | custom-call | tf_op jit(solution)/shard_map/exchange_2/pallas_call | solution.py:195
  138.3 1.3 copy-done.2
  139.6 2.7 %reduce_sum.148 = bf16[64,2048]{1,0:T(8,128)(2,1)} reduce(bf16[8,64,2048]{2,1,0:T(8,128)(2,1)} %copy-done.2, bf16[]{:T(256)} %constant.27.clone.1), dimensions={0}, to_apply=%region_6.0 | reduce | flops 917504 | bytes 2359298 | tf_op jit(solution)/shard_map/reduce_sum | solution.py:293
  142.3 1.5 multiply_reduce_fusion.2
  143.9 1.4 multiply_convert_fusion.1
  145.3 0.8 fusion.1
  146.0 0.8 fusion.2
  146.8 0.4 copy-done.13
  147.3 2.0 pad_maximum_fusion.refs_0_
  149.3 1.0 copy-done.11
  150.3 0.7 fusion.5
  151.2 0.7 fusion.9
  151.9 2.1 add_convert_fusion.refs_1_
  154.0 75.9 %exchange_3.1 = (f32[1,3,512,256]{3,2,1,0:T(8,128)S(1)}, bf16[8,64,2048]{2,1,0:T(8,128)(2,1)S(1)}, f32[1,256,512]{2,1,0:T(8,128)S(1)}) custom-call(bf16[3,2048,256]{2,1,0:T(8,128)(2,1)} %pad_maximum_fusion.refs_0_, bf16[512,2048]{1,0:T(8,128)(2,1)} %add_convert_fusion.refs_1_, bf16[256,2048]{1,0:T(8,128)(2,1)S(1)} %convolution_convert_fusion.1.refs_2_), custom_call_target="tpu_custom_call" | custom-call | tf_op jit(solution)/shard_map/exchange_3/pallas_call | solution.py:195
  230.9 0.9 fusion.26
  231.7 1.1 copy.22
  232.9 0.8 copy.23
  (56 shorter events, 2.6 us)
Async XLA Ops:
  0.6 77.5 %copy-start = (bf16[256,2048]{1,0:T(8,128)(2,1)S(1)}, bf16[256,2048]{1,0:T(8,128)(2,1)}, u32[]{:S(2)}) copy-start(bf16[256,2048]{1,0:T(8,128)(2,1)} %param.12) | copy-start | bytes 3145732
  0.6 3.9 %copy-start.9 = (bf16[64,2048]{1,0:T(8,128)(2,1)S(1)}, bf16[64,2048]{1,0:T(8,128)(2,1)}, u32[]{:S(2)}) copy-start(bf16[64,2048]{1,0:T(8,128)(2,1)} %param.7) | copy-start | bytes 786436
  2.5 29.3 %copy-start.17 = (f32[64]{0:T(128)}, f32[64]{0:T(128)S(1)}, u32[]{:S(2)}) copy-start(f32[64]{0:T(128)S(1)} %add_rsqrt_fusion.4) | copy-start | bytes 772
  2.6 29.3 %copy-start.10 = (bf16[3,2048,256]{2,1,0:T(8,128)(2,1)S(1)}, bf16[3,2048,256]{2,1,0:T(8,128)(2,1)}, u32[]{:S(2)}) copy-start(bf16[3,2048,256]{2,1,0:T(8,128)(2,1)} %param.10) | copy-start | bytes 9437188
  31.8 61.9 %copy-start.3 = (bf16[8,64,2048]{2,1,0:T(8,128)(2,1)}, bf16[8,64,2048]{2,1,0:T(8,128)(2,1)S(1)}, u32[]{:S(2)}) copy-start(bf16[8,64,2048]{2,1,0:T(8,128)(2,1)S(1)} %exchange_0.1) | copy-start | bytes 6291460
  33.3 1.2 copy-start.8
  33.8 1.9 copy-start.7
  76.8 1.3 copy-start.1
  91.3 1.7 copy-start.12
  93.8 1.8 copy-start.15
  93.8 1.8 copy-start.14
  95.6 2.0 copy-start.5
  95.6 2.0 copy-start.6
  138.3 1.3 copy-start.2
  142.3 2.9 %copy-start.4 = (bf16[8,64,2048]{2,1,0:T(8,128)(2,1)S(1)}, bf16[8,64,2048]{2,1,0:T(8,128)(2,1)}, u32[]{:S(2)}) copy-start(bf16[8,64,2048]{2,1,0:T(8,128)(2,1)} %copy-done.3) | copy-start | bytes 6291460
  146.0 1.2 copy-start.13
  147.2 3.0 %copy-start.11 = (bf16[3,2048,256]{2,1,0:T(8,128)(2,1)S(1)}, bf16[3,2048,256]{2,1,0:T(8,128)(2,1)}, u32[]{:S(2)}) copy-start(bf16[3,2048,256]{2,1,0:T(8,128)(2,1)} %param.10) | copy-start | bytes 9437188
  150.3 0.9 copy-start.16
  230.0 0.6 copy-start.18
where the time goes:
time: 234 us
  Pallas kernels  196 us (84%)
  other arithmetic  14.7 us (6%)
  matrix products  14.2 us (6%)
  local copies, waits for them, and re-layouts  6.45 us (3%)
    pallas_call x4, Pallas kernels, exchange(): pl.pallas_call(functools.partial(exchange_kernel, tuple(plan)), out_shape...  185 us
    pallas_call x1, Pallas kernels, attention(): pl.pallas_call(attention_kernel, grid=(heads, span // size), out_shape=[j...  11.7 us
    unnamed x40, local copies, waits for them, and re-layouts  6.45 us
    dot_general x4, matrix products, dot_rows(): lax.dot_general(left, right, (((1,), (1,)), ((), ())), preferred_element_...  5.04 us
    dot_general x4, matrix products, dot_columns(): lax.dot_general(left, right, (((0,), (0,)), ((), ())), preferred_element_...  5.03 us

commit v1 on v0

--- a/solution.py
+++ b/solution.py
@@ -255,11 +255,11 @@
 
     @pl.when(block == pl.num_programs(1) - 1)
     def _():
-        dk_ref[...] = dk_sum[...].astype(jnp.bfloat16)
-        dv_ref[...] = dv_sum[...].astype(jnp.bfloat16)
-
-
-def attention(attn_scale, queries, keys_values, grads):
+        dk_ref[...] = dk_sum[...].astype(dk_ref.dtype)
+        dv_ref[...] = dv_sum[...].astype(dv_ref.dtype)
+
+
+def attention(attn_scale, queries, keys_values, grads, sums=jnp.bfloat16):
     heads = attn_scale.shape[0]
     span, inner = queries.shape
     length = keys_values.shape[0]
@@ -276,8 +276,8 @@
         out_shape=[
             jax.ShapeDtypeStruct((span, inner), jnp.bfloat16),
             jax.ShapeDtypeStruct((span, inner), jnp.float32),
-            jax.ShapeDtypeStruct((length, inner), jnp.bfloat16),
-            jax.ShapeDtypeStruct((length, inner), jnp.bfloat16),
+            jax.ShapeDtypeStruct((length, inner), sums),
+            jax.ShapeDtypeStruct((length, inner), sums),
         ],
         in_specs=[pl.BlockSpec(memory_space=pltpu.SMEM), mine, keys, values, mine],
         out_specs=[mine, mine, keys, keys],
@@ -355,6 +355,364 @@
     return (update, grad_tokens, grad_qkv, grad_out)
 
 
+def flip(index, bit):
+    return index + bit - 2 * bit * ((index // bit) % 2)
+
+
+class Place:
+    def __init__(self):
+        self.row = lax.axis_index("row")
+        self.col = lax.axis_index("col")
+        self.partner = flip(self.col, 1)
+        self.beside = flip(self.col, 2)
+        self.across = flip(self.col, 4)
+        self.corner = flip(self.beside, 4)
+        self.inner = ((self.row + 1) // 2) % 2 == 1
+        self.mate = flip(self.row, 1)
+        self.facing = 3 - self.row
+        low = 1 - self.row // 2
+        self.ranks = [self.row, self.mate, 1 + low, 3 * low]
+
+    def greet(self):
+        barrier = pltpu.get_barrier_semaphore()
+        for peer in (self.partner, self.beside, self.across):
+            pl.semaphore_signal(barrier, inc=1, device_id={"col": peer}, device_id_type=MESH)
+        pl.semaphore_signal(barrier, inc=1, device_id={"row": self.mate}, device_id_type=MESH)
+
+        @pl.when(self.inner)
+        def _():
+            pl.semaphore_signal(
+                barrier, inc=1, device_id={"row": self.facing}, device_id_type=MESH
+            )
+
+        pl.semaphore_wait(barrier, 4 + ((self.row + 1) // 2) % 2)
+
+
+KINDS = 9
+LINE, BESIDE, ACROSS, TOP, BOTTOM, MATE = 0, 1, 2, 3, 4, 5
+SENDS = 12
+
+
+class Gather:
+    def __init__(self, place, job, tile, whole, send_sem, recv_sem):
+        self.place, self.job, self.tile, self.whole = place, job, tile, whole
+        self.send_sem, self.recv_sem = send_sem, recv_sem
+
+    def slot(self, rank, col):
+        return self.whole.at[self.place.ranks[rank], col]
+
+    def link(self, rank, kind, send, source, landing, peer):
+        return pltpu.make_async_remote_copy(
+            src_ref=source,
+            dst_ref=landing,
+            send_sem=self.send_sem.at[self.job, send[0], send[1]],
+            recv_sem=self.recv_sem.at[self.job, rank, kind],
+            device_id=peer,
+            device_id_type=MESH,
+        )
+
+    def arrived(self, rank, kind, landing):
+        self.link(rank, kind, (0, 0), landing, landing, {"col": self.place.partner}).wait_recv()
+
+    def held(self, rank):
+        return self.tile if rank == 0 else self.slot(rank, self.place.col)
+
+    def line_sends(self, rank):
+        p = self.place
+        mine = self.slot(rank, p.col)
+        held = self.held(rank)
+        if rank == 0:
+            outward = self.link(1, LINE, (0, 0), held, mine, {"row": p.mate})
+            inward = self.link(2, LINE, (0, 1), held, mine, {"row": p.facing})
+            return [(outward, False), (inward, True)]
+        if rank == 1:
+            return [(self.link(3, LINE, (1, 0), held, mine, {"row": p.facing}), True)]
+        return [(self.link(rank, LINE, (rank, 0), held, mine, {"row": p.mate}), True)]
+
+    def plane_sends(self, rank):
+        p = self.place
+        mine, held = self.slot(rank, p.col), self.held(rank)
+        return [
+            self.link(rank, BESIDE, (rank, 2), held, mine, {"col": p.beside}),
+            self.link(rank, ACROSS, (rank, 3), held, mine, {"col": p.across}),
+            self.link(rank, MATE, (rank, 4), held, mine, {"col": p.partner}),
+        ]
+
+    def relays(self, rank):
+        p = self.place
+        side, over = self.slot(rank, p.beside), self.slot(rank, p.across)
+        return [
+            self.link(rank, TOP, (rank, 5), half(side, 0), half(side, 0), {"col": p.across}),
+            self.link(rank, MATE + 1, (rank, 6), side, side, {"col": p.partner}),
+            self.link(rank, BOTTOM, (rank, 7), half(over, 1), half(over, 1), {"col": p.beside}),
+            self.link(rank, MATE + 2, (rank, 8), over, over, {"col": p.partner}),
+        ]
+
+    def last(self, rank):
+        p = self.place
+        far = self.slot(rank, p.corner)
+        return self.link(rank, MATE + 3, (rank, 9), far, far, {"col": p.partner})
+
+    def each(self, copies, act):
+        for copy, inner in copies:
+            if inner:
+                pl.when(self.place.inner)(functools.partial(act, copy))
+            else:
+                act(copy)
+
+    def open(self, rank):
+        p = self.place
+        if rank == 0:
+            self.whole[p.row, p.col] = self.tile[...]
+        else:
+            self.arrived(rank, LINE, self.slot(rank, p.col))
+            self.each(self.line_sends(rank), lambda copy: copy.start())
+        for copy in self.plane_sends(rank):
+            copy.start()
+
+    def relay(self, rank):
+        p = self.place
+        top, side, bottom, over = self.relays(rank)
+        self.arrived(rank, BESIDE, self.slot(rank, p.beside))
+        top.start()
+        side.start()
+        self.arrived(rank, ACROSS, self.slot(rank, p.across))
+        bottom.start()
+        over.start()
+
+    def close(self, rank):
+        p = self.place
+        far = self.slot(rank, p.corner)
+        self.arrived(rank, TOP, half(far, 0))
+        self.arrived(rank, BOTTOM, half(far, 1))
+        self.last(rank).start()
+
+    def whole_rank(self, rank):
+        p = self.place
+        for kind, col in enumerate((p.col, p.beside, p.across, p.corner)):
+            self.arrived(rank, MATE + kind, self.slot(rank, flip(col, 1)))
+
+    def drain(self):
+        for rank in range(4):
+            self.each(self.line_sends(rank), lambda copy: copy.wait_send())
+            for copy in self.plane_sends(rank) + self.relays(rank) + [self.last(rank)]:
+                copy.wait_send()
+
+
+def gather_kernel(count, *refs):
+    tiles, wholes = refs[:count], refs[count : 2 * count]
+    send_sem, recv_sem = refs[2 * count :]
+    place = Place()
+    place.greet()
+    jobs = [
+        Gather(place, job, tiles[job], wholes[job], send_sem, recv_sem) for job in range(count)
+    ]
+    for job in jobs:
+        job.each(job.line_sends(0), lambda copy: copy.start())
+    steps = [(job, rank) for job in jobs for rank in range(4)]
+    for at in range(len(steps) + 3):
+        if at < len(steps):
+            steps[at][0].open(steps[at][1])
+        if 0 <= at - 1 < len(steps):
+            steps[at - 1][0].relay(steps[at - 1][1])
+        if 0 <= at - 2 < len(steps):
+            steps[at - 2][0].close(steps[at - 2][1])
+        if 0 <= at - 3 < len(steps):
+            steps[at - 3][0].whole_rank(steps[at - 3][1])
+    for job in jobs:
+        job.drain()
+
+
+def gather_all(tiles, collective_id):
+    count = len(tiles)
+    rows, cols = lax.axis_size("row"), lax.axis_size("col")
+    in_vmem = pl.BlockSpec(memory_space=pltpu.VMEM)
+    return pl.pallas_call(
+        functools.partial(gather_kernel, count),
+        out_shape=[jax.ShapeDtypeStruct((rows, cols) + t.shape, t.dtype) for t in tiles],
+        in_specs=[in_vmem] * count,
+        out_specs=[in_vmem] * count,
+        scratch_shapes=[
+            pltpu.SemaphoreType.DMA((count, 4, SENDS)),
+            pltpu.SemaphoreType.DMA((count, 4, KINDS)),
+        ],
+        compiler_params=pltpu.CompilerParams(
+            collective_id=collective_id, has_side_effects=True, vmem_limit_bytes=48 * 2**20
+        ),
+        name="gather_all",
+    )(*tiles)
+
+
+class Scatter:
+    def __init__(self, place, job, part, crossed, staged, landed, send_sem, recv_sem):
+        self.place, self.job, self.part = place, job, part
+        self.crossed, self.staged, self.landed = crossed, staged, landed
+        self.send_sem, self.recv_sem = send_sem, recv_sem
+        self.size = part.shape[0] // 8
+
+    def targets(self):
+        p = self.place
+        return (p.corner, p.beside, p.across, p.col)
+
+    def rows(self, col):
+        return pl.ds(pl.multiple_of(col * self.size, 16), self.size)
+
+    def core_send(self, at):
+        p = self.place
+        return pltpu.make_async_remote_copy(
+            src_ref=self.part.at[self.rows(flip(self.targets()[at], 1))],
+            dst_ref=self.crossed.at[self.job, at],
+            send_sem=self.send_sem.at[self.job, at],
+            recv_sem=self.recv_sem.at[self.job, at],
+            device_id={"col": p.partner},
+            device_id_type=MESH,
+        )
+
+    def chip_send(self, at):
+        return pltpu.make_async_remote_copy(
+            src_ref=self.staged.at[self.job, at],
+            dst_ref=self.landed.at[self.job, at],
+            send_sem=self.send_sem.at[self.job, 4 + at],
+            recv_sem=self.recv_sem.at[self.job, 4 + at],
+            device_id={"col": self.targets()[at]},
+            device_id_type=MESH,
+        )
+
+    def chip_sum(self, at):
+        mine = self.part[self.rows(self.targets()[at]), :].astype(jnp.float32)
+        return mine + self.crossed[self.job, at].astype(jnp.float32)
+
+    def first(self):
+        for at in range(4):
+            self.core_send(at).start()
+
+    def second(self):
+        for at in range(3):
+            self.core_send(at).wait_recv()
+            self.staged[self.job, at] = self.chip_sum(at).astype(self.staged.dtype)
+            self.chip_send(at).start()
+
+    def third(self):
+        self.core_send(3).wait_recv()
+        total = self.chip_sum(3)
+        for at in (1, 2, 0):
+            self.chip_send(at).wait_recv()
+            total = total + self.landed[self.job, at].astype(jnp.float32)
+        for at in range(4):
+            self.core_send(at).wait_send()
+        for at in range(3):
+            self.chip_send(at).wait_send()
+        return total
+
+
+def greet_plane(place):
+    barrier = pltpu.get_barrier_semaphore()
+    peers = (place.partner, place.beside, place.across, place.corner)
+    for peer in peers:
+        pl.semaphore_signal(barrier, inc=1, device_id={"col": peer}, device_id_type=MESH)
+    pl.semaphore_wait(barrier, len(peers))
+
+
+def scatter_kernel(count, *refs):
+    parts, totals = refs[:count], refs[count : 2 * count]
+    crossed, staged, landed, send_sem, recv_sem = refs[2 * count :]
+    place = Place()
+    greet_plane(place)
+    jobs = [
+        Scatter(place, job, parts[job], crossed, staged, landed, send_sem, recv_sem)
+        for job in range(count)
+    ]
+    for job in jobs:
+        job.first()
+    for job in jobs:
+        job.second()
+    for job, total in zip(jobs, totals):
+        total[...] = job.third()
+
+
+def scatter(parts, collective_id):
+    count = len(parts)
+    rows, width = parts[0].shape
+    size = rows // lax.axis_size("col")
+    in_vmem = pl.BlockSpec(memory_space=pltpu.VMEM)
+    return pl.pallas_call(
+        functools.partial(scatter_kernel, count),
+        out_shape=[jax.ShapeDtypeStruct((size, width), jnp.float32)] * count,
+        in_specs=[in_vmem] * count,
+        out_specs=[in_vmem] * count,
+        scratch_shapes=[
+            pltpu.VMEM((count, 4, size, width), jnp.bfloat16),
+            pltpu.VMEM((count, 3, size, width), jnp.bfloat16),
+            pltpu.VMEM((count, 3, size, width), jnp.bfloat16),
+            pltpu.SemaphoreType.DMA((count, 8)),
+            pltpu.SemaphoreType.DMA((count, 8)),
+        ],
+        compiler_params=pltpu.CompilerParams(
+            collective_id=collective_id, has_side_effects=True, vmem_limit_bytes=48 * 2**20
+        ),
+        name=f"scatter_{collective_id}",
+    )(*parts)
+
+
+def gathered(tokens, timestep, mod_weight, qkv_weight, attn_scale, out_weight, grad_update):
+    tok_dev, width = tokens.shape
+    heads_here = attn_scale.shape[0]
+    inner = qkv_weight.shape[2]
+    head_dim = inner // heads_here
+    rows = lax.axis_size("row")
+    span = tok_dev * lax.axis_size("col")
+    row = lax.axis_index("row")
+    embedded = embed(timestep, mod_weight.shape[0] // 2)
+    gain = 1.0 + jnp.sum(embedded[:, None] * mod_weight, 0)
+    tok_float = tokens.astype(jnp.float32)
+    rstd = lax.rsqrt(jnp.mean(tok_float * tok_float, -1, keepdims=True) + epsilon)
+    normed = tok_float * rstd
+    hidden = (normed * gain).astype(jnp.bfloat16)
+    all_hidden, all_grads = gather_all([hidden, grad_update], 4)
+    all_hidden = all_hidden.reshape(-1, width)
+    all_grads = all_grads.reshape(-1, width)
+    raw = [
+        jnp.dot(all_hidden, qkv_weight[k], preferred_element_type=jnp.float32) for k in range(3)
+    ]
+    query_unit, query_factor = zip(*[unit_rows(part) for part in by_head(raw[0], head_dim)])
+    key_unit, key_factor = zip(*[unit_rows(part) for part in by_head(raw[1], head_dim)])
+    queries = jnp.concatenate(query_unit, 1).astype(jnp.bfloat16)
+    keys_values = jnp.concatenate(key_unit + (raw[2],), 1).astype(jnp.bfloat16)
+    grad_attended = dot_rows(all_grads, out_weight).astype(jnp.bfloat16)
+    attended, grad_query, grad_key, grad_value = attention(
+        attn_scale, queries, keys_values, grad_attended, jnp.float32
+    )
+
+    def of_row(array, dim):
+        size = array.shape[dim] // rows
+        return lax.dynamic_slice_in_dim(array, row * size, size, dim)
+
+    update_part = jnp.dot(
+        of_row(attended, 0), out_weight, preferred_element_type=jnp.float32
+    ).astype(jnp.bfloat16)
+    grad_out = dot_columns(attended, of_row(all_grads, 1))
+
+    def raw_grads(grad_unit, unit, factor):
+        parts = zip(by_head(grad_unit, head_dim), unit, factor)
+        return jnp.concatenate([unit_grad(*part) for part in parts], 1).astype(jnp.bfloat16)
+
+    grad_raw = [
+        raw_grads(grad_query, query_unit, query_factor),
+        raw_grads(grad_key, key_unit, key_factor),
+        grad_value.astype(jnp.bfloat16),
+    ]
+    grad_qkv = jnp.stack([dot_columns(of_row(all_hidden, 1), part) for part in grad_raw])
+    hidden_part = (
+        sum(dot_rows(of_row(part, 0), qkv_weight[k]) for k, part in enumerate(grad_raw))
+    ).astype(jnp.bfloat16)
+    update, grad_hidden = scatter([update_part, hidden_part], 5)
+    grad_normed = grad_hidden * gain
+    grad_tokens = (
+        rstd * (grad_normed - normed * jnp.mean(grad_normed * normed, -1, keepdims=True))
+    ).astype(jnp.bfloat16)
+    return (update.astype(jnp.bfloat16), grad_tokens, grad_qkv, grad_out)
+
+
 def solution(mesh):
     placed = (
         P(("row", "col"), None),
@@ -365,8 +723,9 @@
         P("col", None),
         P(("row", "col"), None),
     )
+    plane = mesh.shape["row"] == 4 and mesh.shape["col"] == 8
     return jax.shard_map(
-        per_device,
+        gathered if plane else per_device,
         mesh=mesh,
         in_specs=placed,
         out_specs=(

time: 234 us -> 206 us (0.88)
  Pallas kernels: 196 us -> 154 us
  matrix products: 14.2 us -> 28.4 us
  local copies, waits for them, and re-layouts: 6.45 us -> 1.88 us
  other arithmetic: 14.7 us -> 19.1 us
    pallas_call x4 -> x2, Pallas kernels: 185 us -> 114 us  [the longest x1 85.6 us: gather_all(): pl.pallas_call(functools.partial(gather_kernel, count), out_shape=[jax.Sh...]
    pallas_call x1, Pallas kernels: 11.7 us -> 40.3 us  [attention(): pl.pallas_call(attention_kernel, grid=(heads, span // size), out_shape=[j...]
    dot_general x4, matrix products: 4.14 us -> 11.8 us  [the longest x3 11.1 us: gathered(): jnp.dot(all_hidden, qkv_weight[k], preferred_element_type=jnp.float32)]
    dot_general x4, matrix products: 5.03 us -> 10.9 us  [dot_columns(): lax.dot_general(left, right, (((0,), (0,)), ((), ())), preferred_element_...]
    unnamed x40 -> x30, local copies, waits for them, and re-layouts: 6.45 us -> 1.88 us
    reduce_sum x5 -> x3, other arithmetic: 6.37 us -> 2.2 us  [the longest x1 1.81 us: gathered(): gain = 1.0 + jnp.sum(embedded[:, None] * mod_weight, 0)]
    another operation x5, other arithmetic: 4.12 us -> 7.2 us
where the time goes in v1:
time: 206 us; the launch traced here: 205 us
  Pallas kernels  154 us (75%)
  matrix products  28.4 us (14%)
  other arithmetic  19.1 us (9%)
    pallas_call x1, Pallas kernels, gather_all(): pl.pallas_call(functools.partial(gather_kernel, count), out_shape=[jax.Sh...  85.6 us
    pallas_call x1, Pallas kernels, attention(): pl.pallas_call(attention_kernel, grid=(heads, span // size), out_shape=[j...  40.3 us
    pallas_call x1, Pallas kernels, scatter(): pl.pallas_call(functools.partial(scatter_kernel, count), out_shape=[jax.S...  28.4 us
    dot_general x3, matrix products, gathered(): jnp.dot(all_hidden, qkv_weight[k], preferred_element_type=jnp.float32)  11.1 us
    dot_general x4, matrix products, dot_columns(): lax.dot_general(left, right, (((0,), (0,)), ((), ())), preferred_element_...  10.9 us
    another operation x4, other arithmetic  5.95 us
    dot_general x4, matrix products, dot_rows(): lax.dot_general(left, right, (((1,), (1,)), ((), ())), preferred_element_...  5.75 us

profile of v1, /device:TPU:0, one launch (start us, length us, event | category | flops | bytes accessed | tf_op | source)
XLA Modules:
  0.0 205.5 jit_solution(5452752966375954052)
XLA Ops:
  1.5 1.8 multiply_reduce_fusion
  3.7 85.6 %gather_all.1 = (bf16[4,8,64,2048]{3,2,1,0:T(8,128)(2,1)}, bf16[4,8,64,2048]{3,2,1,0:T(8,128)(2,1)}) custom-call(bf16[64,2048]{1,0:T(8,128)(2,1)S(1)} %fusion.40.refs_0_, bf16[64,2048]{1,0:T(8,128)(2,1)S(1)} %copy-done.1), custom_call_target="tpu_custom_call" | custom-call | tf_op jit(solution)/shard_map/gather_all/pallas_call | solution.py:530
  89.3 6.1 %fusion.21 = f32[2048,256]{1,0:T(8,128)S(1)} fusion(bf16[2048,2048]{1,0:T(8,128)(2,1)} %bitcast.32, bf16[3,2048,256]{2,1,0:T(8,128)(2,1)} %param.10), kind=kOutput, calls=%fused_computation.29 | convolution fusion | flops 2147483648 | bytes 11534336 | tf_op jit(solution)/shard_map/dot_general | solution.py:675
  95.4 0.6 multiply_reduce_fusion.6
  96.0 0.9 fusion.35
  97.0 0.9 copy-done.5
  97.9 2.5 %convolution_convert_fusion.2 = bf16[2048,256]{1,0:T(8,128)(2,1)S(1)} fusion(bf16[2048,2048]{1,0:T(8,128)(2,1)S(1)} %bitcast.38, bf16[3,2048,256]{2,1,0:T(8,128)(2,1)S(1)} %copy-done.5), kind=kOutput, calls=%fused_computation.3 | convolution fusion | flops 2148007936 | bytes 10485760 | tf_op jit(solution)/shard_map/dot_general | solution.py:675
  100.4 1.5 pad_maximum_fusion.k_ref.v_ref
  101.9 2.5 %fusion.25 = f32[2048,256]{1,0:T(8,128)S(1)} fusion(bf16[2048,2048]{1,0:T(8,128)(2,1)S(1)} %bitcast.39, bf16[3,2048,256]{2,1,0:T(8,128)(2,1)S(1)} %copy-done.5), kind=kOutput, calls=%fused_computation.33 | convolution fusion | flops 2147483648 | bytes 11534336 | tf_op jit(solution)/shard_map/dot_general | solution.py:675
  104.4 0.6 multiply_reduce_fusion.8
  105.0 0.7 fusion.33
  105.8 1.1 pad_maximum_fusion.6.q_ref
  106.9 3.5 %convolution_convert_fusion.1.g_ref = bf16[2048,256]{1,0:T(8,128)(2,1)} fusion(bf16[2048,2048]{1,0:T(8,128)(2,1)S(1)} %bitcast.43, bf16[256,2048]{1,0:T(8,128)(2,1)S(1)} %copy-done), kind=kOutput, calls=%fused_computation.2 | convolution fusion | flops 2148007936 | bytes 10485760 | tf_op jit(solution)/shard_map/dot_general | solution.py:214
  110.4 40.3 %attention.1 = (bf16[2048,256]{1,0:T(8,128)(2,1)}, f32[2048,256]{1,0:T(8,128)}, f32[2048,256]{1,0:T(8,128)}, f32[2048,256]{1,0:T(8,128)}) custom-call(f32[2]{0:T(128)} %scale_ref.1, bf16[2048,256]{1,0:T(8,128)(2,1)} %pad_maximum_fusion.6.q_ref, bf16[2048,512]{1,0:T(8,128)(2,1)} %pad_maximum_fusion.k_ref.v_ref, ...), custom_call_target="tpu_custom_call" | custom-call | tf_op jit(solution)/shard_map/attention/pallas_call | solution.py:273
  150.7 2.6 %multiply_reduce_fusion.3 = (f32[2048]{0:T(1024)S(1)}, f32[2048]{0:T(1024)S(1)}) fusion(f32[2048,256]{1,0:T(8,128)} %get-tuple-element.15, f32[2048,256]{1,0:T(8,128)S(1)} %fusion.25, f32[2048]{0:T(1024)S(1)} %add_rsqrt_fusion.2, f32[2048]{0:T(1024)S(1)} %add_rsqrt_fusion.3), kind=kLoop, calls=%fused_computation.40 | loop fusion | flops 1568768 | bytes 4227072 | tf_op jit(solution)/shard_map/reduce_sum | solution.py:33
  153.4 2.7 %multiply_convert_fusion.2 = (bf16[2048,128]{1,0:T(8,128)(2,1)}, bf16[2048,128]{1,0:T(8,128)(2,1)}) fusion(f32[2048,256]{1,0:T(8,128)S(1)} %copy-done.3, f32[2048,256]{1,0:T(8,128)S(1)} %fusion.25, f32[2048]{0:T(1024)S(1)} %broadcast_multiply_fusion.2, f32[2048]{0:T(1024)S(1)} %add_rsqrt_fusion.2, f32[2048]{0:T(1024)S(1)} %broadcast_multiply_fusion.3, ...), kind=kLoop, calls=%fused_computation.39 | loop fusion | flops 2621440 | bytes 5275648 | tf_op jit(solution)/shard_map/convert.3
  156.1 2.7 %fusion.8 = f32[1,512,256]{2,1,0:T(8,128)S(1)} fusion(bf16[2048,2048]{1,0:T(8,128)(2,1)} %bitcast.33, s32[]{:T(128)S(6)} %select_n.2, bf16[2048,128]{1,0:T(8,128)(2,1)} %get-tuple-element.30, bf16[2048,128]{1,0:T(8,128)(2,1)} %get-tuple-element.31), kind=kOutput, calls=%fused_computation.15 | convolution fusion | flops 538968064 | bytes 3670020 | tf_op jit(solution)/shard_map/dot_general | solution.py:220
  158.9 1.3 multiply_reduce_fusion.1
  160.2 1.6 multiply_convert_fusion
  161.8 2.5 %fusion.11 = f32[1,512,256]{2,1,0:T(8,128)S(1)} fusion(bf16[2048,2048]{1,0:T(8,128)(2,1)} %bitcast.34, s32[]{:T(128)S(6)} %select_n.2, bf16[2048,128]{1,0:T(8,128)(2,1)S(1)} %get-tuple-element.28, bf16[2048,128]{1,0:T(8,128)(2,1)S(1)} %get-tuple-element.29), kind=kOutput, calls=%fused_computation.16 | convolution fusion | flops 538968064 | bytes 3670020 | tf_op jit(solution)/shard_map/dot_general | solution.py:220
  164.5 2.3 %fusion.14 = f32[1,512,256]{2,1,0:T(8,128)S(1)} fusion(bf16[2048,256]{1,0:T(8,128)(2,1)S(1)} %convert_element_type.36, bf16[2048,2048]{1,0:T(8,128)(2,1)} %bitcast.35, s32[]{:T(128)S(6)} %select_n.2), kind=kOutput, calls=%fused_computation.17 | convolution fusion | flops 536870912 | bytes 3670020 | tf_op jit(solution)/shard_map/dot_general | solution.py:220
  166.8 1.2 pad_maximum_fusion.1
  168.1 0.4 copy-done.10
  168.5 3.3 %fusion = f32[256,512]{1,0:T(8,128)} fusion(bf16[2048,256]{1,0:T(8,128)(2,1)S(1)} %copy-done.10, bf16[2048,2048]{1,0:T(8,128)(2,1)} %bitcast.40, s32[]{:T(128)S(6)} %select_n.2), kind=kOutput, calls=%fused_computation.5 | convolution fusion | flops 536870912 | bytes 3670020 | tf_op jit(solution)/shard_map/dot_general | solution.py:220
  171.9 0.7 fusion.19
  172.6 0.3 copy-done.7
  173.0 0.7 fusion.23
  173.8 0.7 add_convert_fusion.refs_1_
  174.6 0.7 convolution_convert_fusion.refs_0_
  175.3 28.4 %scatter_5.1 = (f32[64,2048]{1,0:T(8,128)S(1)}, f32[64,2048]{1,0:T(8,128)S(1)}) custom-call(bf16[512,2048]{1,0:T(8,128)(2,1)S(1)} %convolution_convert_fusion.refs_0_, bf16[512,2048]{1,0:T(8,128)(2,1)S(1)} %add_convert_fusion.refs_1_), custom_call_target="tpu_custom_call" | custom-call | tf_op jit(solution)/shard_map/scatter_5/pallas_call | solution.py:638
  203.9 0.9 fusion.44
  204.8 0.7 convert_element_type.38
  (46 shorter events, 1.0 us)
Async XLA Ops:
  0.6 106.2 %copy-start = (bf16[256,2048]{1,0:T(8,128)(2,1)S(1)}, bf16[256,2048]{1,0:T(8,128)(2,1)}, u32[]{:S(2)}) copy-start(bf16[256,2048]{1,0:T(8,128)(2,1)} %param.12) | copy-start | bytes 3145732
  0.6 2.7 %copy-start.4 = (bf16[64,2048]{1,0:T(8,128)(2,1)S(1)}, bf16[64,2048]{1,0:T(8,128)(2,1)}, u32[]{:S(2)}) copy-start(bf16[64,2048]{1,0:T(8,128)(2,1)} %param.7) | copy-start | bytes 786436
  0.7 3.0 %copy-start.1 = (bf16[64,2048]{1,0:T(8,128)(2,1)S(1)}, bf16[64,2048]{1,0:T(8,128)(2,1)}, u32[]{:S(2)}) copy-start(bf16[64,2048]{1,0:T(8,128)(2,1)} %refs_1_.1) | copy-start | bytes 786436
  89.2 7.7 %slice-start = ((s8[8388608]{0:T(1024)(128)(4,1)}), s8[4194304]{0:T(1024)(128)(4,1)S(1)}, s32[]{:S(2)}) async-start(s8[8388608]{0:T(1024)(128)(4,1)} %bitcast.36), calls=%async_computation | async-start | bytes 8388608
  89.2 7.7 %slice-start.1 = ((s8[8388608]{0:T(1024)(128)(4,1)}), s8[4194304]{0:T(1024)(128)(4,1)S(1)}, s32[]{:S(2)}) async-start(s8[8388608]{0:T(1024)(128)(4,1)} %bitcast.36), calls=%async_computation.1 | async-start | bytes 8388608
  96.0 1.9 copy-start.5
  100.4 6.5 %slice-start.2 = ((s8[8388608]{0:T(1024)(128)(4,1)}), s8[4194304]{0:T(1024)(128)(4,1)S(1)}, s32[]{:S(2)}) async-start(s8[8388608]{0:T(1024)(128)(4,1)} %bitcast.41), calls=%async_computation.2 | async-start | bytes 8388608
  101.9 4.9 %slice-start.3 = ((s8[8388608]{0:T(1024)(128)(4,1)}), s8[4194304]{0:T(1024)(128)(4,1)S(1)}, s32[]{:S(2)}) async-start(s8[8388608]{0:T(1024)(128)(4,1)} %bitcast.41), calls=%async_computation.3 | async-start | bytes 8388608
  150.7 2.7 %copy-start.3 = (f32[2048,256]{1,0:T(8,128)S(1)}, f32[2048,256]{1,0:T(8,128)}, u32[]{:S(2)}) copy-start(f32[2048,256]{1,0:T(8,128)} %get-tuple-element.15) | copy-start | bytes 6291460
  156.1 2.7 %copy-start.2 = (f32[2048,256]{1,0:T(8,128)S(1)}, f32[2048,256]{1,0:T(8,128)}, u32[]{:S(2)}) copy-start(f32[2048,256]{1,0:T(8,128)} %get-tuple-element.16) | copy-start | bytes 6291460
  161.8 2.5 %copy-start.9 = (f32[2048,256]{1,0:T(8,128)S(1)}, f32[2048,256]{1,0:T(8,128)}, u32[]{:S(2)}) copy-start(f32[2048,256]{1,0:T(8,128)} %get-tuple-element.17) | copy-start | bytes 6291460
  166.8 1.7 copy-start.10
  168.1 3.8 %copy-start.6 = (bf16[3,2048,256]{2,1,0:T(8,128)(2,1)S(1)}, bf16[3,2048,256]{2,1,0:T(8,128)(2,1)}, u32[]{:S(2)}) copy-start(bf16[3,2048,256]{2,1,0:T(8,128)(2,1)} %param.10) | copy-start | bytes 9437188
  171.8 1.0 copy-start.7
  171.8 1.2 copy-start.8

commit v2 on v1

--- a/solution.py
+++ b/solution.py
@@ -259,7 +259,7 @@
         dv_ref[...] = dv_sum[...].astype(dv_ref.dtype)
 
 
-def attention(attn_scale, queries, keys_values, grads, sums=jnp.bfloat16):
+def attention(attn_scale, queries, keys_values, grads):
     heads = attn_scale.shape[0]
     span, inner = queries.shape
     length = keys_values.shape[0]
@@ -276,8 +276,8 @@
         out_shape=[
             jax.ShapeDtypeStruct((span, inner), jnp.bfloat16),
             jax.ShapeDtypeStruct((span, inner), jnp.float32),
-            jax.ShapeDtypeStruct((length, inner), sums),
-            jax.ShapeDtypeStruct((length, inner), sums),
+            jax.ShapeDtypeStruct((length, inner), jnp.bfloat16),
+            jax.ShapeDtypeStruct((length, inner), jnp.bfloat16),
         ],
         in_specs=[pl.BlockSpec(memory_space=pltpu.SMEM), mine, keys, values, mine],
         out_specs=[mine, mine, keys, keys],
@@ -375,7 +375,7 @@
 
     def greet(self):
         barrier = pltpu.get_barrier_semaphore()
-        for peer in (self.partner, self.beside, self.across):
+        for peer in (self.partner, self.beside, self.across, self.corner):
             pl.semaphore_signal(barrier, inc=1, device_id={"col": peer}, device_id_type=MESH)
         pl.semaphore_signal(barrier, inc=1, device_id={"row": self.mate}, device_id_type=MESH)
 
@@ -385,7 +385,7 @@
                 barrier, inc=1, device_id={"row": self.facing}, device_id_type=MESH
             )
 
-        pl.semaphore_wait(barrier, 4 + ((self.row + 1) // 2) % 2)
+        pl.semaphore_wait(barrier, 5 + ((self.row + 1) // 2) % 2)
 
 
 KINDS = 9
@@ -499,50 +499,6 @@
                 copy.wait_send()
 
 
-def gather_kernel(count, *refs):
-    tiles, wholes = refs[:count], refs[count : 2 * count]
-    send_sem, recv_sem = refs[2 * count :]
-    place = Place()
-    place.greet()
-    jobs = [
-        Gather(place, job, tiles[job], wholes[job], send_sem, recv_sem) for job in range(count)
-    ]
-    for job in jobs:
-        job.each(job.line_sends(0), lambda copy: copy.start())
-    steps = [(job, rank) for job in jobs for rank in range(4)]
-    for at in range(len(steps) + 3):
-        if at < len(steps):
-            steps[at][0].open(steps[at][1])
-        if 0 <= at - 1 < len(steps):
-            steps[at - 1][0].relay(steps[at - 1][1])
-        if 0 <= at - 2 < len(steps):
-            steps[at - 2][0].close(steps[at - 2][1])
-        if 0 <= at - 3 < len(steps):
-            steps[at - 3][0].whole_rank(steps[at - 3][1])
-    for job in jobs:
-        job.drain()
-
-
-def gather_all(tiles, collective_id):
-    count = len(tiles)
-    rows, cols = lax.axis_size("row"), lax.axis_size("col")
-    in_vmem = pl.BlockSpec(memory_space=pltpu.VMEM)
-    return pl.pallas_call(
-        functools.partial(gather_kernel, count),
-        out_shape=[jax.ShapeDtypeStruct((rows, cols) + t.shape, t.dtype) for t in tiles],
-        in_specs=[in_vmem] * count,
-        out_specs=[in_vmem] * count,
-        scratch_shapes=[
-            pltpu.SemaphoreType.DMA((count, 4, SENDS)),
-            pltpu.SemaphoreType.DMA((count, 4, KINDS)),
-        ],
-        compiler_params=pltpu.CompilerParams(
-            collective_id=collective_id, has_side_effects=True, vmem_limit_bytes=48 * 2**20
-        ),
-        name="gather_all",
-    )(*tiles)
-
-
 class Scatter:
     def __init__(self, place, job, part, crossed, staged, landed, send_sem, recv_sem):
         self.place, self.job, self.part = place, job, part
@@ -605,107 +561,317 @@
         return total
 
 
-def greet_plane(place):
-    barrier = pltpu.get_barrier_semaphore()
-    peers = (place.partner, place.beside, place.across, place.corner)
-    for peer in peers:
-        pl.semaphore_signal(barrier, inc=1, device_id={"col": peer}, device_id_type=MESH)
-    pl.semaphore_wait(barrier, len(peers))
-
-
-def scatter_kernel(count, *refs):
-    parts, totals = refs[:count], refs[count : 2 * count]
-    crossed, staged, landed, send_sem, recv_sem = refs[2 * count :]
+LOG2E = 1.4426950408889634
+
+
+def dot(left, right):
+    return jnp.dot(left, right, preferred_element_type=jnp.float32)
+
+
+def fused_kernel(
+    scale_ref, hidden_ref, grad_ref, qkv_ref, out_ref,
+    update_ref, down_ref, grad_qkv_ref, grad_out_ref,
+    hid_all, grad_all, raw_ref, q_ref, k_ref, kt_ref, v_ref, vt_ref, do_ref, w_ref,
+    att_ref, dkt_ref, dvt_ref, gr_ref,
+    part_ref, crossed, staged, landed, send_sem, recv_sem, send_sum, recv_sum,
+):
+    bf = jnp.bfloat16
     place = Place()
-    greet_plane(place)
-    jobs = [
-        Scatter(place, job, parts[job], crossed, staged, landed, send_sem, recv_sem)
-        for job in range(count)
+    rows, cols, tok_dev, width = hid_all.shape
+    heads, length, hdim = q_ref.shape
+    span = cols * tok_dev
+    size = w_ref.shape[0]
+    per_rank = span // size
+    narrow = width // rows
+    place.greet()
+    hid = Gather(place, 0, hidden_ref, hid_all, send_sem, recv_sem)
+    grd = Gather(place, 1, grad_ref, grad_all, send_sem, recv_sem)
+    scatters = [
+        Scatter(place, job, part_ref.at[job], crossed, staged, landed, send_sum, recv_sum)
+        for job in range(2)
     ]
-    for job in jobs:
-        job.first()
-    for job in jobs:
-        job.second()
-    for job, total in zip(jobs, totals):
-        total[...] = job.third()
-
-
-def scatter(parts, collective_id):
-    count = len(parts)
-    rows, width = parts[0].shape
-    size = rows // lax.axis_size("col")
+
+    def start_all(copies):
+        hid.each(copies, lambda copy: copy.start())
+
+    def tokens_at(rank, chunk):
+        return pl.multiple_of(place.ranks[rank] * span + chunk * size, size)
+
+    def chunk_of(whole, rank, chunk):
+        step = size // tok_dev
+        picked = whole[place.ranks[rank], pl.ds(chunk * step, step)]
+        return picked.reshape(size, width)
+
+    def project(rank):
+        def body(chunk, carry):
+            at = pl.ds(tokens_at(rank, chunk), size)
+            here = chunk_of(hid_all, rank, chunk)
+            for k in range(3):
+                raw = dot(here, qkv_ref[k])
+                for head, part in enumerate(by_head(raw, hdim)):
+                    if k < 2:
+                        raw_ref[k, head, at, :] = part
+                        part = unit_rows(part)[0]
+                    part = part.astype(bf)
+                    if k == 0:
+                        q_ref[head, at, :] = part
+                    elif k == 1:
+                        k_ref[head, at, :] = part
+                        kt_ref[head, :, at] = part.T
+                    else:
+                        v_ref[head, at, pl.ds(0, hdim)] = part
+                        vt_ref[head, pl.ds(0, hdim), at] = part.T
+            return carry
+
+        lax.fori_loop(0, per_rank, body, 0)
+
+    def cotangent(rank):
+        def body(chunk, carry):
+            value = dot_rows(chunk_of(grad_all, rank, chunk), out_ref[...]).astype(bf)
+            for head, part in enumerate(by_head(value, hdim)):
+                do_ref[head, pl.ds(pl.multiple_of(chunk * size, size), size), :] = part
+            return carry
+
+        lax.fori_loop(0, per_rank, body, 0)
+
+    wide = min(512, length)
+    lane = lax.broadcasted_iota(jnp.int32, (size, hdim), 1)
+
+    def attend(rank):
+        def body(step, carry):
+            head = step // per_rank
+            chunk = step % per_rank
+            at = pl.ds(tokens_at(rank, chunk), size)
+            scale = scale_ref[head]
+            coeff = scale * (1.0 / hdim)
+            query = q_ref[head, at, :]
+            grad = do_ref[head, pl.ds(pl.multiple_of(chunk * size, size), size), :]
+            mixed = None
+            for start in range(0, length, wide):
+                scores = dot(query, kt_ref[head, :, pl.ds(start, wide)])
+                weights = jnp.exp2(scores * (coeff * LOG2E)).astype(bf)
+                w_ref[:, pl.ds(start, wide)] = weights
+                more = dot(weights, v_ref[head, pl.ds(start, wide), :])
+                mixed = more if mixed is None else mixed + more
+            inverse = 1.0 / mixed[:, hdim : hdim + 1]
+            attended = (mixed[:, :hdim] * inverse).astype(bf)
+            att_ref[head, at, :] = attended
+            grad_float = grad.astype(jnp.float32)
+            delta = jnp.sum(grad_float * attended.astype(jnp.float32), -1, keepdims=True)
+            high = delta.astype(bf).astype(jnp.float32)
+            spare = jnp.where(lane == 0, -high, jnp.where(lane == 1, high - delta, 0.0))
+            grad_more = jnp.concatenate([grad, spare.astype(bf)], 1)
+            grad_turned = (grad_float * inverse).T.astype(bf)
+            query_turned = (query.astype(jnp.float32) * (inverse * coeff)).T.astype(bf)
+            grad_query = None
+            for start in range(0, length, wide):
+                here = pl.ds(start, wide)
+                weights = w_ref[:, here]
+                dprobs = dot(grad_more, vt_ref[head, :, here])
+                dscores = weights * dprobs.astype(bf)
+                more = dot(dscores, k_ref[head, here, :])
+                grad_query = more if grad_query is None else grad_query + more
+                dkt_ref[head, :, here] += dot(query_turned, dscores)
+                dvt_ref[head, :, here] += dot(grad_turned, weights)
+            unit, factor = unit_rows(raw_ref[0, head, at, :])
+            gr_ref[0, head, at, :] = unit_grad(
+                grad_query * (inverse * coeff), unit, factor
+            ).astype(bf)
+            return carry
+
+        lax.fori_loop(0, heads * per_rank, body, 0)
+
+    def finish_keys(rank):
+        def body(step, carry):
+            head = step // per_rank
+            at = pl.ds(tokens_at(rank, step % per_rank), size)
+            unit, factor = unit_rows(raw_ref[1, head, at, :])
+            gr_ref[1, head, at, :] = unit_grad(dkt_ref[head, :, at].T, unit, factor).astype(bf)
+            gr_ref[2, head, at, :] = dvt_ref[head, :, at].T.astype(bf)
+            return carry
+
+        lax.fori_loop(0, heads * per_rank, body, 0)
+
+    own = pl.multiple_of(place.row * span, span)
+
+    def project_out():
+        def body(chunk, carry):
+            at = pl.ds(pl.multiple_of(own + chunk * size, size), size)
+            mine = jnp.concatenate([att_ref[head, at, :] for head in range(heads)], 1)
+            part_ref[0, pl.ds(pl.multiple_of(chunk * size, size), size), :] = dot(
+                mine, out_ref[...]
+            ).astype(bf)
+            return carry
+
+        lax.fori_loop(0, per_rank, body, 0)
+
+    def project_down():
+        def body(chunk, carry):
+            at = pl.ds(pl.multiple_of(own + chunk * size, size), size)
+            total = None
+            for k in range(3):
+                mine = jnp.concatenate([gr_ref[k, head, at, :] for head in range(heads)], 1)
+                more = dot_rows(mine, qkv_ref[k])
+                total = more if total is None else total + more
+            part_ref[1, pl.ds(pl.multiple_of(chunk * size, size), size), :] = total.astype(bf)
+            return carry
+
+        lax.fori_loop(0, per_rank, body, 0)
+
+    def columns(whole, start, count):
+        at = pl.multiple_of(place.row * narrow + start, 128)
+        return whole[:, :, :, pl.ds(at, count)].reshape(length, count)
+
+    def weight_grads():
+        few = 128
+
+        def body(step, carry):
+            start = pl.multiple_of(step * few, few)
+            turned = columns(hid_all, start, few).T
+            for k in range(3):
+                for head in range(heads):
+                    grad_qkv_ref[k, pl.ds(start, few), pl.ds(head * hdim, hdim)] = dot(
+                        turned, gr_ref[k, head]
+                    )
+            return carry
+
+        lax.fori_loop(0, narrow // few, body, 0)
+
+    def out_grads():
+        for head in range(heads):
+            turned = att_ref[head].T
+            grad_out_ref[pl.ds(head * hdim, hdim), :] = dot(turned, columns(grad_all, 0, narrow))
+
+    start_all(hid.line_sends(0))
+    hid.open(0)
+    v_ref[:, :, pl.ds(hdim, hdim)] = jnp.ones((heads, length, hdim), bf)
+    vt_ref[:, pl.ds(hdim, hdim), :] = jnp.ones((heads, hdim, length), bf)
+    dkt_ref[...] = jnp.zeros_like(dkt_ref)
+    dvt_ref[...] = jnp.zeros_like(dvt_ref)
+    hid.open(1)
+    hid.relay(0)
+    hid.open(2)
+    start_all(grd.line_sends(0))
+    hid.relay(1)
+    hid.close(0)
+    hid.whole_rank(0)
+    project(0)
+    hid.open(3)
+    hid.relay(2)
+    hid.close(1)
+    hid.whole_rank(1)
+    grd.open(0)
+    project(1)
+    hid.relay(3)
+    hid.close(2)
+    hid.whole_rank(2)
+    grd.open(1)
+    project(2)
+    hid.close(3)
+    hid.whole_rank(3)
+    grd.relay(0)
+    project(3)
+    grd.open(2)
+    grd.relay(1)
+    grd.close(0)
+    grd.whole_rank(0)
+    cotangent(0)
+    attend(0)
+    grd.open(3)
+    grd.relay(2)
+    grd.close(1)
+    grd.whole_rank(1)
+    project_out()
+    scatters[0].first()
+    cotangent(1)
+    attend(1)
+    grd.relay(3)
+    grd.close(2)
+    grd.whole_rank(2)
+    scatters[0].second()
+    cotangent(2)
+    attend(2)
+    grd.close(3)
+    grd.whole_rank(3)
+    cotangent(3)
+    attend(3)
+    finish_keys(0)
+    project_down()
+    scatters[1].first()
+    for rank in range(1, 4):
+        finish_keys(rank)
+    scatters[1].second()
+    weight_grads()
+    out_grads()
+    update_ref[...] = scatters[0].third()
+    down_ref[...] = scatters[1].third()
+    hid.drain()
+    grd.drain()
+
+
+def fused(scale, hidden, grad_update, qkv_weight, out_weight):
+    bf, f32 = jnp.bfloat16, jnp.float32
+    tok_dev, width = hidden.shape
+    heads = scale.shape[0]
+    inner = qkv_weight.shape[2]
+    hdim = inner // heads
+    rows, cols = lax.axis_size("row"), lax.axis_size("col")
+    span = tok_dev * cols
+    length = span * rows
+    size = math.gcd(span, 256)
+    narrow = width // rows
     in_vmem = pl.BlockSpec(memory_space=pltpu.VMEM)
     return pl.pallas_call(
-        functools.partial(scatter_kernel, count),
-        out_shape=[jax.ShapeDtypeStruct((size, width), jnp.float32)] * count,
-        in_specs=[in_vmem] * count,
-        out_specs=[in_vmem] * count,
+        fused_kernel,
+        out_shape=[
+            jax.ShapeDtypeStruct((tok_dev, width), f32),
+            jax.ShapeDtypeStruct((tok_dev, width), f32),
+            jax.ShapeDtypeStruct((3, narrow, inner), f32),
+            jax.ShapeDtypeStruct((inner, narrow), f32),
+        ],
+        in_specs=[pl.BlockSpec(memory_space=pltpu.SMEM)] + [in_vmem] * 4,
+        out_specs=[in_vmem] * 4,
         scratch_shapes=[
-            pltpu.VMEM((count, 4, size, width), jnp.bfloat16),
-            pltpu.VMEM((count, 3, size, width), jnp.bfloat16),
-            pltpu.VMEM((count, 3, size, width), jnp.bfloat16),
-            pltpu.SemaphoreType.DMA((count, 8)),
-            pltpu.SemaphoreType.DMA((count, 8)),
+            pltpu.VMEM((rows, cols, tok_dev, width), bf),
+            pltpu.VMEM((rows, cols, tok_dev, width), bf),
+            pltpu.VMEM((2, heads, length, hdim), f32),
+            pltpu.VMEM((heads, length, hdim), bf),
+            pltpu.VMEM((heads, length, hdim), bf),
+            pltpu.VMEM((heads, hdim, length), bf),
+            pltpu.VMEM((heads, length, 2 * hdim), bf),
+            pltpu.VMEM((heads, 2 * hdim, length), bf),
+            pltpu.VMEM((heads, span, hdim), bf),
+            pltpu.VMEM((size, length), bf),
+            pltpu.VMEM((heads, length, hdim), bf),
+            pltpu.VMEM((heads, hdim, length), f32),
+            pltpu.VMEM((heads, hdim, length), f32),
+            pltpu.VMEM((3, heads, length, hdim), bf),
+            pltpu.VMEM((2, span, width), bf),
+            pltpu.VMEM((2, 4, tok_dev, width), bf),
+            pltpu.VMEM((2, 3, tok_dev, width), bf),
+            pltpu.VMEM((2, 3, tok_dev, width), bf),
+            pltpu.SemaphoreType.DMA((2, 4, SENDS)),
+            pltpu.SemaphoreType.DMA((2, 4, KINDS)),
+            pltpu.SemaphoreType.DMA((2, 8)),
+            pltpu.SemaphoreType.DMA((2, 8)),
         ],
         compiler_params=pltpu.CompilerParams(
-            collective_id=collective_id, has_side_effects=True, vmem_limit_bytes=48 * 2**20
+            collective_id=4, has_side_effects=True, vmem_limit_bytes=60 * 2**20
         ),
-        name=f"scatter_{collective_id}",
-    )(*parts)
+        name="fused",
+    )(scale, hidden, grad_update, qkv_weight, out_weight)
 
 
 def gathered(tokens, timestep, mod_weight, qkv_weight, attn_scale, out_weight, grad_update):
-    tok_dev, width = tokens.shape
-    heads_here = attn_scale.shape[0]
-    inner = qkv_weight.shape[2]
-    head_dim = inner // heads_here
-    rows = lax.axis_size("row")
-    span = tok_dev * lax.axis_size("col")
-    row = lax.axis_index("row")
     embedded = embed(timestep, mod_weight.shape[0] // 2)
     gain = 1.0 + jnp.sum(embedded[:, None] * mod_weight, 0)
     tok_float = tokens.astype(jnp.float32)
     rstd = lax.rsqrt(jnp.mean(tok_float * tok_float, -1, keepdims=True) + epsilon)
     normed = tok_float * rstd
     hidden = (normed * gain).astype(jnp.bfloat16)
-    all_hidden, all_grads = gather_all([hidden, grad_update], 4)
-    all_hidden = all_hidden.reshape(-1, width)
-    all_grads = all_grads.reshape(-1, width)
-    raw = [
-        jnp.dot(all_hidden, qkv_weight[k], preferred_element_type=jnp.float32) for k in range(3)
-    ]
-    query_unit, query_factor = zip(*[unit_rows(part) for part in by_head(raw[0], head_dim)])
-    key_unit, key_factor = zip(*[unit_rows(part) for part in by_head(raw[1], head_dim)])
-    queries = jnp.concatenate(query_unit, 1).astype(jnp.bfloat16)
-    keys_values = jnp.concatenate(key_unit + (raw[2],), 1).astype(jnp.bfloat16)
-    grad_attended = dot_rows(all_grads, out_weight).astype(jnp.bfloat16)
-    attended, grad_query, grad_key, grad_value = attention(
-        attn_scale, queries, keys_values, grad_attended, jnp.float32
-    )
-
-    def of_row(array, dim):
-        size = array.shape[dim] // rows
-        return lax.dynamic_slice_in_dim(array, row * size, size, dim)
-
-    update_part = jnp.dot(
-        of_row(attended, 0), out_weight, preferred_element_type=jnp.float32
-    ).astype(jnp.bfloat16)
-    grad_out = dot_columns(attended, of_row(all_grads, 1))
-
-    def raw_grads(grad_unit, unit, factor):
-        parts = zip(by_head(grad_unit, head_dim), unit, factor)
-        return jnp.concatenate([unit_grad(*part) for part in parts], 1).astype(jnp.bfloat16)
-
-    grad_raw = [
-        raw_grads(grad_query, query_unit, query_factor),
-        raw_grads(grad_key, key_unit, key_factor),
-        grad_value.astype(jnp.bfloat16),
-    ]
-    grad_qkv = jnp.stack([dot_columns(of_row(all_hidden, 1), part) for part in grad_raw])
-    hidden_part = (
-        sum(dot_rows(of_row(part, 0), qkv_weight[k]) for k, part in enumerate(grad_raw))
-    ).astype(jnp.bfloat16)
-    update, grad_hidden = scatter([update_part, hidden_part], 5)
+    update, grad_hidden, grad_qkv, grad_out = fused(
+        attn_scale, hidden, grad_update, qkv_weight, out_weight
+    )
     grad_normed = grad_hidden * gain
     grad_tokens = (
         rstd * (grad_normed - normed * jnp.mean(grad_normed * normed, -1, keepdims=True))

time: 206 us -> 151 us (0.73)
  matrix products: 28.4 us -> 0 us
  Pallas kernels: 154 us -> 139 us
  other arithmetic: 19.1 us -> 8.96 us
    dot_general x12 -> x0, matrix products: 28.5 us -> none  [the longest x3 11.1 us: gathered(): jnp.dot(all_hidden, qkv_weight[k], preferred_element_type=jnp.float32)]
    pallas_call x3 -> x1, Pallas kernels: 154 us -> 139 us  [fused(): pl.pallas_call(fused_kernel, out_shape=[jax.ShapeDtypeStruct((tok_dev, wi...]
    another operation x5 -> x0, other arithmetic: 7.2 us -> none
    reduce_sum x4 -> x0, other arithmetic: 5.17 us -> none  [the longest x2 3.94 us: unit_grad(): jnp.mean(grad_unit * unit, -1, keepdims=True)]
    concatenate x2 -> x0, other arithmetic: 2.61 us -> none  [the longest x1 1.52 us: gathered(): keys_values = jnp.concatenate(key_unit + (raw[2],), 1).astype(jnp.bfloat16)]
where the time goes in v2:
time: 151 us
  Pallas kernels  139 us (92%)
  other arithmetic  8.96 us (6%)
  local copies, waits for them, and re-layouts  1.95 us (1%)
    pallas_call x1, Pallas kernels, fused(): pl.pallas_call(fused_kernel, out_shape=[jax.ShapeDtypeStruct((tok_dev, wi...  139 us

profile of v2, /device:TPU:0, one launch (start us, length us, event | category | flops | bytes accessed | tf_op | source)
XLA Modules:
  0.0 151.0 jit_solution(17532934386911917977)
XLA Ops:
  0.6 0.0 copy-start
  1.3 1.1 fusion.8
  2.4 0.1 fusion.9
  2.5 1.8 %multiply_reduce_fusion = f32[2048]{0:T(1024)S(1)} fusion(f32[256,2048]{1,0:T(8,128)} %param.9, f32[256]{0:T(256)S(1)} %pad_maximum_fusion), kind=kLoop, calls=%fused_computation | loop fusion | flops 1046528 | bytes 2106368 | tf_op jit(solution)/shard_map/reduce_sum | solution.py:867
  4.4 0.0 copy-done
  4.4 0.8 fusion.3.hidden_ref
  5.2 138.7 %fused.1 = (f32[64,2048]{1,0:T(8,128)}, f32[64,2048]{1,0:T(8,128)}, f32[3,512,256]{2,1,0:T(8,128)}, f32[256,512]{1,0:T(8,128)}) custom-call(f32[2]{0:T(128)} %scale_ref.1, bf16[64,2048]{1,0:T(8,128)(2,1)} %fusion.3.hidden_ref, bf16[64,2048]{1,0:T(8,128)(2,1)} %grad_ref.1, bf16[3,2048,256]{2,1,0:T(8,128)(2,1)} %qkv_ref.1, bf16[256,2048]{1,0:T(8,128)(2,1)} %out_ref.1), custom_call_target="tpu_custom_call" | custom-call | tf_op jit(solution)/shard_map/fused/pallas_call | solution.py:824
  143.9 0.0 copy-start.1
  143.9 1.9 %convert_element_type.18 = bf16[64,2048]{1,0:T(8,128)(2,1)} convert(f32[64,2048]{1,0:T(8,128)} %get-tuple-element.8) | non-fusion elementwise | flops 131072 | bytes 786432 | tf_op jit(solution)/shard_map/convert_element_type | solution.py:879
  145.8 1.3 fusion.4
  147.1 0.0 copy-start.2
  147.1 2.0 %fusion.7 = bf16[64,2048]{1,0:T(8,128)(2,1)} fusion(bf16[64,2048]{1,0:T(8,128)(2,1)S(1)} %copy-done, f32[64,2048]{1,0:T(8,128)} %get-tuple-element.9, f32[64]{0:T(128)S(1)} %broadcast_multiply_fusion, f32[2048]{0:T(1024)S(1)} %broadcast_add_fusion, f32[64]{0:T(128)S(1)} %add_rsqrt_fusion), kind=kLoop, calls=%fused_computation.10 | loop fusion | flops 917504 | bytes 1057280 | tf_op jit(solution)/shard_map/convert_element_type | solution.py:878
  149.1 0.0 copy-done.1
  149.1 1.1 copy.14
  150.2 0.0 copy-done.2
  150.2 0.8 copy.15
  (4 shorter events, 0.0 us)
Async XLA Ops:
  0.6 3.7 %copy-start = (bf16[64,2048]{1,0:T(8,128)(2,1)S(1)}, bf16[64,2048]{1,0:T(8,128)(2,1)}, u32[]{:S(2)}) copy-start(bf16[64,2048]{1,0:T(8,128)(2,1)} %param.7) | copy-start | bytes 786436
  143.9 5.2 %copy-start.1 = (f32[3,512,256]{2,1,0:T(8,128)S(1)}, f32[3,512,256]{2,1,0:T(8,128)}, u32[]{:S(2)}) copy-start(f32[3,512,256]{2,1,0:T(8,128)} %get-tuple-element.20) | copy-start | bytes 4718596
  147.1 3.1 %copy-start.2 = (f32[256,512]{1,0:T(8,128)S(1)}, f32[256,512]{1,0:T(8,128)}, u32[]{:S(2)}) copy-start(f32[256,512]{1,0:T(8,128)} %get-tuple-element.21) | copy-start | bytes 1572868

commit v3 on v2

--- a/solution.py
+++ b/solution.py
@@ -377,15 +377,11 @@
         barrier = pltpu.get_barrier_semaphore()
         for peer in (self.partner, self.beside, self.across, self.corner):
             pl.semaphore_signal(barrier, inc=1, device_id={"col": peer}, device_id_type=MESH)
-        pl.semaphore_signal(barrier, inc=1, device_id={"row": self.mate}, device_id_type=MESH)
-
-        @pl.when(self.inner)
-        def _():
-            pl.semaphore_signal(
-                barrier, inc=1, device_id={"row": self.facing}, device_id_type=MESH
-            )
-
-        pl.semaphore_wait(barrier, 5 + ((self.row + 1) // 2) % 2)
+        for peer in self.ranks[1:]:
+            pl.semaphore_signal(barrier, inc=1, device_id={"row": peer}, device_id_type=MESH)
+
+    def await_greetings(self):
+        pl.semaphore_wait(pltpu.get_barrier_semaphore(), 7)
 
 
 KINDS = 9
@@ -460,13 +456,11 @@
             else:
                 act(copy)
 
-    def open(self, rank):
-        p = self.place
-        if rank == 0:
-            self.whole[p.row, p.col] = self.tile[...]
-        else:
-            self.arrived(rank, LINE, self.slot(rank, p.col))
-            self.each(self.line_sends(rank), lambda copy: copy.start())
+    def pass_on(self, rank):
+        self.arrived(rank, LINE, self.slot(rank, self.place.col))
+        self.each(self.line_sends(rank), lambda copy: copy.start())
+
+    def spread(self, rank):
         for copy in self.plane_sends(rank):
             copy.start()
 
@@ -492,17 +486,64 @@
         for kind, col in enumerate((p.col, p.beside, p.across, p.corner)):
             self.arrived(rank, MATE + kind, self.slot(rank, flip(col, 1)))
 
-    def drain(self):
+    def drain_line(self):
         for rank in range(4):
             self.each(self.line_sends(rank), lambda copy: copy.wait_send())
-            for copy in self.plane_sends(rank) + self.relays(rank) + [self.last(rank)]:
-                copy.wait_send()
+
+    def drain_plane(self, rank):
+        for copy in self.plane_sends(rank) + self.relays(rank) + [self.last(rank)]:
+            copy.wait_send()
+
+
+class Level(Gather):
+    def slot(self, rank, col):
+        return self.whole.at[col]
+
+
+class Line(Gather):
+    def slot(self, rank, col):
+        return self.whole.at[self.place.ranks[rank]]
+
+
+class Slices(Gather):
+    def cuts(self):
+        p = self.place
+        size = self.whole.shape[3]
+        copies = []
+        for at, peer in enumerate(p.ranks[1:]):
+            mine = pl.ds(pl.multiple_of(peer * size, 128), size)
+            copies.append(
+                pltpu.make_async_remote_copy(
+                    src_ref=self.tile.at[:, mine],
+                    dst_ref=self.slot(0, p.col),
+                    send_sem=self.send_sem.at[self.job, at, 0],
+                    recv_sem=self.recv_sem.at[self.job, p.row, LINE],
+                    device_id={"row": peer},
+                    device_id_type=MESH,
+                )
+            )
+        return copies
+
+    def landed(self, rank):
+        p = self.place
+        slot = self.slot(rank, p.col)
+        pltpu.make_async_remote_copy(
+            src_ref=slot,
+            dst_ref=slot,
+            send_sem=self.send_sem.at[self.job, 0, 0],
+            recv_sem=self.recv_sem.at[self.job, p.ranks[rank], LINE],
+            device_id={"col": p.partner},
+            device_id_type=MESH,
+        ).wait_recv()
+
+    def held(self, rank):
+        return self.slot(rank, self.place.col)
 
 
 class Scatter:
-    def __init__(self, place, job, part, crossed, staged, landed, send_sem, recv_sem):
+    def __init__(self, place, job, part, crossed, landed, send_sem, recv_sem):
         self.place, self.job, self.part = place, job, part
-        self.crossed, self.staged, self.landed = crossed, staged, landed
+        self.crossed, self.landed = crossed, landed
         self.send_sem, self.recv_sem = send_sem, recv_sem
         self.size = part.shape[0] // 8
 
@@ -526,7 +567,7 @@
 
     def chip_send(self, at):
         return pltpu.make_async_remote_copy(
-            src_ref=self.staged.at[self.job, at],
+            src_ref=self.part.at[self.rows(self.targets()[at])],
             dst_ref=self.landed.at[self.job, at],
             send_sem=self.send_sem.at[self.job, 4 + at],
             recv_sem=self.recv_sem.at[self.job, 4 + at],
@@ -545,7 +586,7 @@
     def second(self):
         for at in range(3):
             self.core_send(at).wait_recv()
-            self.staged[self.job, at] = self.chip_sum(at).astype(self.staged.dtype)
+            self.part[self.rows(self.targets()[at]), :] = self.chip_sum(at).astype(self.part.dtype)
             self.chip_send(at).start()
 
     def third(self):
@@ -569,26 +610,54 @@
 
 
 def fused_kernel(
-    scale_ref, hidden_ref, grad_ref, qkv_ref, out_ref,
-    update_ref, down_ref, grad_qkv_ref, grad_out_ref,
-    hid_all, grad_all, raw_ref, q_ref, k_ref, kt_ref, v_ref, vt_ref, do_ref, w_ref,
-    att_ref, dkt_ref, dvt_ref, gr_ref,
-    part_ref, crossed, staged, landed, send_sem, recv_sem, send_sum, recv_sum,
+    scale_ref, embed_ref, tok_ref, grad_ref, mod_hbm, qkv_hbm, out_hbm,
+    update_ref, grad_tok_ref, grad_qkv_ref, grad_out_ref,
+    hidden_ref, gain_ref, qkv_ref, out_ref, load_sem, hid_all, grad_level, grad_cut, do_all, raw_ref, q_ref, qt_ref, k_ref, kt_ref, v_ref, vt_ref,
+    w_ref, inv_ref, own_ref, att_ref, dot_ref, dkt_ref, dvt_ref, gr_ref,
+    part_ref, crossed, landed, send_sem, recv_sem, send_sum, recv_sum,
 ):
     bf = jnp.bfloat16
     place = Place()
     rows, cols, tok_dev, width = hid_all.shape
     heads, length, hdim = q_ref.shape
     span = cols * tok_dev
-    size = w_ref.shape[0]
+    size = math.gcd(span, 256)
     per_rank = span // size
     narrow = width // rows
+    dog_ref = v_ref
+    mod_loads = [
+        pltpu.make_async_copy(
+            mod_hbm.at[pl.ds(head * hdim, hdim)], dkt_ref.at[head], load_sem.at[2 + head]
+        )
+        for head in range(heads)
+    ]
+    loads = [
+        pltpu.make_async_copy(qkv_hbm, qkv_ref, load_sem.at[0]),
+        pltpu.make_async_copy(out_hbm, out_ref, load_sem.at[1]),
+    ]
+    for load in mod_loads + loads:
+        load.start()
     place.greet()
+    gain = 1.0
+    for head, load in enumerate(mod_loads):
+        load.wait()
+        here = embed_ref[pl.ds(head * hdim, hdim), :] * dkt_ref[head]
+        gain = gain + jnp.sum(here, 0, keepdims=True)
+    gain_ref[...] = jnp.broadcast_to(gain, gain_ref.shape)
+
+    def normed_rows():
+        tok_float = tok_ref[...].astype(jnp.float32)
+        rstd = lax.rsqrt(jnp.mean(tok_float * tok_float, -1, keepdims=True) + epsilon)
+        return tok_float * rstd, rstd
+
+    hidden_ref[...] = (normed_rows()[0] * gain_ref[0:1, :]).astype(bf)
+    place.await_greetings()
     hid = Gather(place, 0, hidden_ref, hid_all, send_sem, recv_sem)
-    grd = Gather(place, 1, grad_ref, grad_all, send_sem, recv_sem)
+    grd = Level(place, 1, grad_ref, grad_level, send_sem, recv_sem)
+    cut = Slices(place, 2, grad_ref, grad_cut, send_sem, recv_sem)
+    dol = Line(place, 3, do_all.at[place.row], do_all, send_sem, recv_sem)
     scatters = [
-        Scatter(place, job, part_ref.at[job], crossed, staged, landed, send_sum, recv_sum)
-        for job in range(2)
+        Scatter(place, job, part_ref, crossed, landed, send_sum, recv_sum) for job in range(2)
     ]
 
     def start_all(copies):
@@ -597,286 +666,414 @@
     def tokens_at(rank, chunk):
         return pl.multiple_of(place.ranks[rank] * span + chunk * size, size)
 
-    def chunk_of(whole, rank, chunk):
-        step = size // tok_dev
-        picked = whole[place.ranks[rank], pl.ds(chunk * step, step)]
-        return picked.reshape(size, width)
+    def within(chunk):
+        return pl.ds(pl.multiple_of(chunk * size, size), size)
+
+    def steps(count, body):
+        def step(at, carry):
+            body(at)
+            return carry
+
+        lax.fori_loop(0, count, step, 0)
+
+    def blocks(body):
+        steps(heads * per_rank, lambda at: body(at // per_rank, at % per_rank))
+
+    few = size // tok_dev
 
     def project(rank):
-        def body(chunk, carry):
+        def body(chunk):
             at = pl.ds(tokens_at(rank, chunk), size)
-            here = chunk_of(hid_all, rank, chunk)
+            here = hid_all[place.ranks[rank], pl.ds(chunk * few, few)].reshape(size, width)
             for k in range(3):
                 raw = dot(here, qkv_ref[k])
                 for head, part in enumerate(by_head(raw, hdim)):
                     if k < 2:
-                        raw_ref[k, head, at, :] = part
+                        raw_ref[k, head, at, :] = part.astype(bf)
                         part = unit_rows(part)[0]
                     part = part.astype(bf)
                     if k == 0:
                         q_ref[head, at, :] = part
+                        qt_ref[head, :, at] = part.T
                     elif k == 1:
                         k_ref[head, at, :] = part
                         kt_ref[head, :, at] = part.T
                     else:
                         v_ref[head, at, pl.ds(0, hdim)] = part
                         vt_ref[head, pl.ds(0, hdim), at] = part.T
-            return carry
-
-        lax.fori_loop(0, per_rank, body, 0)
-
-    def cotangent(rank):
-        def body(chunk, carry):
-            value = dot_rows(chunk_of(grad_all, rank, chunk), out_ref[...]).astype(bf)
+
+        steps(per_rank, body)
+
+    def cotangent():
+        def body(chunk):
+            here = grad_level[pl.ds(chunk * few, few)].reshape(size, width)
+            value = dot_rows(here, out_ref[...]).astype(bf)
             for head, part in enumerate(by_head(value, hdim)):
-                do_ref[head, pl.ds(pl.multiple_of(chunk * size, size), size), :] = part
-            return carry
-
-        lax.fori_loop(0, per_rank, body, 0)
-
-    wide = min(512, length)
-    lane = lax.broadcasted_iota(jnp.int32, (size, hdim), 1)
-
-    def attend(rank):
-        def body(step, carry):
-            head = step // per_rank
-            chunk = step % per_rank
+                do_all[place.row, head, within(chunk), :] = part
+
+        steps(per_rank, body)
+
+    wide = min(512, span)
+
+    def forward(rank):
+        def body(head, chunk):
             at = pl.ds(tokens_at(rank, chunk), size)
-            scale = scale_ref[head]
-            coeff = scale * (1.0 / hdim)
+            coeff = scale_ref[head] * (LOG2E / hdim)
             query = q_ref[head, at, :]
-            grad = do_ref[head, pl.ds(pl.multiple_of(chunk * size, size), size), :]
             mixed = None
             for start in range(0, length, wide):
-                scores = dot(query, kt_ref[head, :, pl.ds(start, wide)])
-                weights = jnp.exp2(scores * (coeff * LOG2E)).astype(bf)
-                w_ref[:, pl.ds(start, wide)] = weights
-                more = dot(weights, v_ref[head, pl.ds(start, wide), :])
+                here = pl.ds(start, wide)
+                weights = jnp.exp2(dot(query, kt_ref[head, :, here]) * coeff).astype(bf)
+                w_ref[head, at, here] = weights
+                more = dot(weights, v_ref[head, here, :])
                 mixed = more if mixed is None else mixed + more
-            inverse = 1.0 / mixed[:, hdim : hdim + 1]
+            inverse = 1.0 / mixed[:, hdim:]
             attended = (mixed[:, :hdim] * inverse).astype(bf)
-            att_ref[head, at, :] = attended
-            grad_float = grad.astype(jnp.float32)
-            delta = jnp.sum(grad_float * attended.astype(jnp.float32), -1, keepdims=True)
+            if rank == 0:
+                own_ref[head, within(chunk), :] = attended
+            att_ref[head, :, at] = attended.T
+            inv_ref[head, :, at] = inverse.T[:8]
+
+        blocks(body)
+
+    def prepare(rank):
+        def body(head, chunk):
+            at = pl.ds(tokens_at(rank, chunk), size)
+            turned = do_all[place.ranks[rank], head, within(chunk), :].T.astype(jnp.float32)
+            delta = jnp.sum(turned * att_ref[head, :, at].astype(jnp.float32), 0, keepdims=True)
+            inverse = inv_ref[head, 0:1, at]
+            turned = turned * inverse
+            dot_ref[head, :, at] = turned.astype(bf)
+            delta = jnp.broadcast_to(delta * inverse, (hdim, size))
             high = delta.astype(bf).astype(jnp.float32)
-            spare = jnp.where(lane == 0, -high, jnp.where(lane == 1, high - delta, 0.0))
-            grad_more = jnp.concatenate([grad, spare.astype(bf)], 1)
-            grad_turned = (grad_float * inverse).T.astype(bf)
-            query_turned = (query.astype(jnp.float32) * (inverse * coeff)).T.astype(bf)
+            line = lax.broadcasted_iota(jnp.int32, (hdim, size), 0)
+            spare = jnp.where(line == 0, -high, jnp.where(line == 1, high - delta, 0.0))
+            dog_ref[head, at, :] = jnp.concatenate([turned, spare], 0).astype(bf).T
+
+        blocks(body)
+
+    def backward(rank, fresh, stored=()):
+        def body(head, chunk):
+            at = pl.ds(tokens_at(rank, chunk), size)
+            coeff = scale_ref[head] * (1.0 / hdim)
+            whole = len(fresh) + len(stored) == rows
+            grad_more = dog_ref[head, at, :]
+            grad_turned = dot_ref[head, :, at]
+            query_turned = qt_ref[head, :, at]
             grad_query = None
-            for start in range(0, length, wide):
-                here = pl.ds(start, wide)
-                weights = w_ref[:, here]
-                dprobs = dot(grad_more, vt_ref[head, :, here])
-                dscores = weights * dprobs.astype(bf)
-                more = dot(dscores, k_ref[head, here, :])
-                grad_query = more if grad_query is None else grad_query + more
-                dkt_ref[head, :, here] += dot(query_turned, dscores)
-                dvt_ref[head, :, here] += dot(grad_turned, weights)
-            unit, factor = unit_rows(raw_ref[0, head, at, :])
-            gr_ref[0, head, at, :] = unit_grad(
-                grad_query * (inverse * coeff), unit, factor
-            ).astype(bf)
-            return carry
-
-        lax.fori_loop(0, heads * per_rank, body, 0)
+            for key_rank in stored + fresh:
+                first = pl.multiple_of(place.ranks[key_rank] * span, span)
+                for start in range(0, span, wide):
+                    here = pl.ds(pl.multiple_of(first + start, wide), wide)
+                    weights = w_ref[head, at, here]
+                    if key_rank in fresh:
+                        dprobs = dot(grad_more, vt_ref[head, :, here])
+                        dscores = weights * dprobs.astype(bf)
+                        dkt_ref[head, :, here] += dot(query_turned, dscores)
+                        dvt_ref[head, :, here] += dot(grad_turned, weights)
+                        if not whole:
+                            w_ref[head, at, here] = dscores
+                    else:
+                        dscores = weights
+                    if whole:
+                        more = dot(dscores, k_ref[head, here, :])
+                        grad_query = more if grad_query is None else grad_query + more
+            if whole:
+                unit, factor = unit_rows(raw_ref[0, head, at, :].astype(jnp.float32))
+                gr_ref[0, head, at, :] = unit_grad(grad_query * coeff, unit, factor).astype(bf)
+
+        blocks(body)
 
     def finish_keys(rank):
-        def body(step, carry):
-            head = step // per_rank
-            at = pl.ds(tokens_at(rank, step % per_rank), size)
-            unit, factor = unit_rows(raw_ref[1, head, at, :])
-            gr_ref[1, head, at, :] = unit_grad(dkt_ref[head, :, at].T, unit, factor).astype(bf)
-            gr_ref[2, head, at, :] = dvt_ref[head, :, at].T.astype(bf)
-            return carry
-
-        lax.fori_loop(0, heads * per_rank, body, 0)
-
-    own = pl.multiple_of(place.row * span, span)
+        def body(head, chunk):
+            at = pl.ds(tokens_at(rank, chunk), size)
+            coeff = scale_ref[head] * (1.0 / hdim)
+            unit, factor = unit_rows(raw_ref[1, head, at, :].astype(jnp.float32))
+            both = jnp.concatenate([dkt_ref[head, :, at], dvt_ref[head, :, at]], 0).astype(bf).T
+            grad_key = both[:, :hdim].astype(jnp.float32) * coeff
+            gr_ref[1, head, at, :] = unit_grad(grad_key, unit, factor).astype(bf)
+            gr_ref[2, head, at, :] = both[:, hdim:]
+
+        blocks(body)
 
     def project_out():
-        def body(chunk, carry):
-            at = pl.ds(pl.multiple_of(own + chunk * size, size), size)
-            mine = jnp.concatenate([att_ref[head, at, :] for head in range(heads)], 1)
-            part_ref[0, pl.ds(pl.multiple_of(chunk * size, size), size), :] = dot(
-                mine, out_ref[...]
-            ).astype(bf)
-            return carry
-
-        lax.fori_loop(0, per_rank, body, 0)
+        def body(chunk):
+            mine = jnp.concatenate([own_ref[h, within(chunk), :] for h in range(heads)], 1)
+            part_ref[within(chunk), :] = dot(mine, out_ref[...]).astype(bf)
+
+        steps(per_rank, body)
 
     def project_down():
-        def body(chunk, carry):
-            at = pl.ds(pl.multiple_of(own + chunk * size, size), size)
+        def body(chunk):
+            at = pl.ds(tokens_at(0, chunk), size)
             total = None
             for k in range(3):
                 mine = jnp.concatenate([gr_ref[k, head, at, :] for head in range(heads)], 1)
                 more = dot_rows(mine, qkv_ref[k])
                 total = more if total is None else total + more
-            part_ref[1, pl.ds(pl.multiple_of(chunk * size, size), size), :] = total.astype(bf)
-            return carry
-
-        lax.fori_loop(0, per_rank, body, 0)
-
-    def columns(whole, start, count):
-        at = pl.multiple_of(place.row * narrow + start, 128)
-        return whole[:, :, :, pl.ds(at, count)].reshape(length, count)
+            part_ref[within(chunk), :] = total.astype(bf)
+
+        steps(per_rank, body)
 
     def weight_grads():
-        few = 128
-
-        def body(step, carry):
-            start = pl.multiple_of(step * few, few)
-            turned = columns(hid_all, start, few).T
+        part = min(256, narrow)
+
+        def body(step):
+            start = pl.multiple_of(step * part, part)
+            at = pl.ds(pl.multiple_of(place.row * narrow + start, 128), part)
+            turned = hid_all[:, :, :, at].reshape(length, part).T
             for k in range(3):
-                for head in range(heads):
-                    grad_qkv_ref[k, pl.ds(start, few), pl.ds(head * hdim, hdim)] = dot(
-                        turned, gr_ref[k, head]
-                    )
-            return carry
-
-        lax.fori_loop(0, narrow // few, body, 0)
+                here = jnp.concatenate([gr_ref[k, head] for head in range(heads)], 1)
+                grad_qkv_ref[k, pl.ds(start, part), :] = dot(turned, here)
+
+        steps(narrow // part, body)
 
     def out_grads():
-        for head in range(heads):
-            turned = att_ref[head].T
-            grad_out_ref[pl.ds(head * hdim, hdim), :] = dot(turned, columns(grad_all, 0, narrow))
+        mine = pl.ds(pl.multiple_of(place.row * narrow, 128), narrow)
+        for rank in range(rows):
+            if rank == 0:
+                here = grad_level[:, :, mine]
+            else:
+                here = grad_cut[place.ranks[rank]]
+            here = here.reshape(span, narrow)
+            at = pl.ds(tokens_at(rank, 0), span)
+            for head in range(heads):
+                more = dot(att_ref[head, :, at], here)
+                to = pl.ds(head * hdim, hdim)
+                if rank == 0:
+                    grad_out_ref[to, :] = more
+                else:
+                    grad_out_ref[to, :] += more
+
+    def tokens_grad(down):
+        normed, rstd = normed_rows()
+        grad_normed = down * gain_ref[0:1, :]
+        pull = jnp.mean(grad_normed * normed, -1, keepdims=True)
+        grad_tok_ref[...] = (rstd * (grad_normed - normed * pull)).astype(bf)
 
     start_all(hid.line_sends(0))
-    hid.open(0)
+    hid.spread(0)
+    hid_all[place.row, place.col] = hidden_ref[...]
     v_ref[:, :, pl.ds(hdim, hdim)] = jnp.ones((heads, length, hdim), bf)
     vt_ref[:, pl.ds(hdim, hdim), :] = jnp.ones((heads, hdim, length), bf)
     dkt_ref[...] = jnp.zeros_like(dkt_ref)
     dvt_ref[...] = jnp.zeros_like(dvt_ref)
-    hid.open(1)
+    grad_level[place.col] = grad_ref[...]
+    hid.pass_on(1)
+    hid.spread(1)
     hid.relay(0)
-    hid.open(2)
-    start_all(grd.line_sends(0))
+    hid.pass_on(2)
+    hid.spread(2)
+
+    @pl.when(place.inner)
+    def _():
+        hid.pass_on(3)
+
     hid.relay(1)
     hid.close(0)
     hid.whole_rank(0)
+    for load in loads:
+        load.wait()
     project(0)
-    hid.open(3)
+
+    @pl.when(jnp.logical_not(place.inner))
+    def _():
+        hid.arrived(3, LINE, hid.slot(3, place.col))
+
+    hid.spread(3)
+    for copy in cut.cuts():
+        copy.start()
     hid.relay(2)
     hid.close(1)
     hid.whole_rank(1)
-    grd.open(0)
     project(1)
     hid.relay(3)
+    grd.spread(0)
     hid.close(2)
     hid.whole_rank(2)
-    grd.open(1)
     project(2)
     hid.close(3)
     hid.whole_rank(3)
+    project(3)
     grd.relay(0)
-    project(3)
-    grd.open(2)
-    grd.relay(1)
+    forward(0)
     grd.close(0)
-    grd.whole_rank(0)
-    cotangent(0)
-    attend(0)
-    grd.open(3)
-    grd.relay(2)
-    grd.close(1)
-    grd.whole_rank(1)
     project_out()
     scatters[0].first()
-    cotangent(1)
-    attend(1)
-    grd.relay(3)
-    grd.close(2)
-    grd.whole_rank(2)
+    grd.whole_rank(0)
+    cotangent()
+    start_all(dol.line_sends(0))
     scatters[0].second()
-    cotangent(2)
-    attend(2)
-    grd.close(3)
-    grd.whole_rank(3)
-    cotangent(3)
-    attend(3)
+    for rank in range(1, 4):
+        cut.landed(rank)
+        cut.spread(rank)
+    forward(1)
+    forward(2)
+    dol.pass_on(1)
+
+    @pl.when(place.inner)
+    def _():
+        dol.pass_on(2)
+
+    forward(3)
+    prepare(0)
+
+    @pl.when(place.inner)
+    def _():
+        dol.pass_on(3)
+
+    backward(0, (0, 1, 2, 3))
+    cut.relay(1)
+    cut.relay(2)
+    prepare(1)
+    backward(1, (0, 1, 2, 3))
+    cut.relay(3)
+    cut.close(1)
+    cut.close(2)
+
+    @pl.when(jnp.logical_not(place.inner))
+    def _():
+        dol.arrived(2, LINE, dol.slot(2, place.col))
+
+    prepare(2)
+    backward(2, (0,))
+    cut.close(3)
+
+    @pl.when(jnp.logical_not(place.inner))
+    def _():
+        dol.arrived(3, LINE, dol.slot(3, place.col))
+
+    prepare(3)
+    backward(3, (0,))
+    update_ref[...] = scatters[0].third().astype(update_ref.dtype)
     finish_keys(0)
     project_down()
     scatters[1].first()
     for rank in range(1, 4):
+        cut.whole_rank(rank)
+    out_grads()
+    scatters[1].second()
+    backward(2, (1, 2, 3), (0,))
+    backward(3, (1, 2, 3), (0,))
+    for rank in range(1, 4):
         finish_keys(rank)
-    scatters[1].second()
     weight_grads()
-    out_grads()
-    update_ref[...] = scatters[0].third()
-    down_ref[...] = scatters[1].third()
-    hid.drain()
-    grd.drain()
-
-
-def fused(scale, hidden, grad_update, qkv_weight, out_weight):
+    tokens_grad(scatters[1].third())
+    hid.drain_line()
+    dol.drain_line()
+    grd.drain_plane(0)
+    for copy in cut.cuts():
+        copy.wait_send()
+    for rank in range(4):
+        hid.drain_plane(rank)
+        if rank > 0:
+            cut.drain_plane(rank)
+
+
+def fused(scale, embedded, tokens, grad_update, mod_weight, qkv_weight, out_weight):
     bf, f32 = jnp.bfloat16, jnp.float32
-    tok_dev, width = hidden.shape
+    tok_dev, width = tokens.shape
     heads = scale.shape[0]
     inner = qkv_weight.shape[2]
     hdim = inner // heads
     rows, cols = lax.axis_size("row"), lax.axis_size("col")
     span = tok_dev * cols
     length = span * rows
-    size = math.gcd(span, 256)
     narrow = width // rows
     in_vmem = pl.BlockSpec(memory_space=pltpu.VMEM)
     return pl.pallas_call(
         fused_kernel,
         out_shape=[
-            jax.ShapeDtypeStruct((tok_dev, width), f32),
-            jax.ShapeDtypeStruct((tok_dev, width), f32),
+            jax.ShapeDtypeStruct((tok_dev, width), bf),
+            jax.ShapeDtypeStruct((tok_dev, width), bf),
             jax.ShapeDtypeStruct((3, narrow, inner), f32),
             jax.ShapeDtypeStruct((inner, narrow), f32),
         ],
-        in_specs=[pl.BlockSpec(memory_space=pltpu.SMEM)] + [in_vmem] * 4,
+        in_specs=[pl.BlockSpec(memory_space=pltpu.SMEM)]
+        + [in_vmem] * 3
+        + [pl.BlockSpec(memory_space=pl.ANY)] * 3,
         out_specs=[in_vmem] * 4,
         scratch_shapes=[
+            pltpu.VMEM((tok_dev, width), bf),
+            pltpu.VMEM((8, width), f32),
+            pltpu.VMEM(qkv_weight.shape, bf),
+            pltpu.VMEM(out_weight.shape, bf),
+            pltpu.SemaphoreType.DMA((2 + heads,)),
             pltpu.VMEM((rows, cols, tok_dev, width), bf),
-            pltpu.VMEM((rows, cols, tok_dev, width), bf),
-            pltpu.VMEM((2, heads, length, hdim), f32),
+            pltpu.VMEM((cols, tok_dev, width), bf),
+            pltpu.VMEM((rows, cols, tok_dev, narrow), bf),
+            pltpu.VMEM((rows, heads, span, hdim), bf),
+            pltpu.VMEM((2, heads, length, hdim), bf),
             pltpu.VMEM((heads, length, hdim), bf),
+            pltpu.VMEM((heads, hdim, length), bf),
             pltpu.VMEM((heads, length, hdim), bf),
             pltpu.VMEM((heads, hdim, length), bf),
             pltpu.VMEM((heads, length, 2 * hdim), bf),
             pltpu.VMEM((heads, 2 * hdim, length), bf),
+            pltpu.VMEM((heads, length, length), bf),
+            pltpu.VMEM((heads, 8, length), f32),
             pltpu.VMEM((heads, span, hdim), bf),
-            pltpu.VMEM((size, length), bf),
-            pltpu.VMEM((heads, length, hdim), bf),
+            pltpu.VMEM((heads, hdim, length), bf),
+            pltpu.VMEM((heads, hdim, length), bf),
             pltpu.VMEM((heads, hdim, length), f32),
             pltpu.VMEM((heads, hdim, length), f32),
             pltpu.VMEM((3, heads, length, hdim), bf),
-            pltpu.VMEM((2, span, width), bf),
+            pltpu.VMEM((span, width), bf),
             pltpu.VMEM((2, 4, tok_dev, width), bf),
             pltpu.VMEM((2, 3, tok_dev, width), bf),
-            pltpu.VMEM((2, 3, tok_dev, width), bf),
-            pltpu.SemaphoreType.DMA((2, 4, SENDS)),
-            pltpu.SemaphoreType.DMA((2, 4, KINDS)),
+            pltpu.SemaphoreType.DMA((4, 4, SENDS)),
+            pltpu.SemaphoreType.DMA((4, 4, KINDS)),
             pltpu.SemaphoreType.DMA((2, 8)),
             pltpu.SemaphoreType.DMA((2, 8)),
         ],
         compiler_params=pltpu.CompilerParams(
-            collective_id=4, has_side_effects=True, vmem_limit_bytes=60 * 2**20
+            collective_id=4, has_side_effects=True, vmem_limit_bytes=67043328
         ),
         name="fused",
-    )(scale, hidden, grad_update, qkv_weight, out_weight)
+    )(scale, embedded, tokens, grad_update, mod_weight, qkv_weight, out_weight)
+
+
+def hand_over_kernel(*refs):
+    count = (len(refs) - 2) // 3
+    given, taken, held = refs[:count], refs[count : 2 * count], refs[2 * count : 3 * count]
+    in_sem, out_sem = refs[3 * count :]
+    ins = [pltpu.make_async_copy(given[n], held[n], in_sem.at[n]) for n in range(count)]
+    outs = [pltpu.make_async_copy(held[n], taken[n], out_sem.at[n]) for n in range(count)]
+    for copy in ins:
+        copy.start()
+    for first, then in zip(ins, outs):
+        first.wait()
+        then.start()
+    for copy in outs:
+        copy.wait()
+
+
+def hand_over(arrays):
+    count = len(arrays)
+    anywhere = pl.BlockSpec(memory_space=pl.ANY)
+    return pl.pallas_call(
+        hand_over_kernel,
+        out_shape=[jax.ShapeDtypeStruct(a.shape, a.dtype) for a in arrays],
+        in_specs=[anywhere] * count,
+        out_specs=[anywhere] * count,
+        scratch_shapes=[pltpu.VMEM(a.shape, a.dtype) for a in arrays]
+        + [pltpu.SemaphoreType.DMA((count,))] * 2,
+        name="hand_over",
+    )(*arrays)
 
 
 def gathered(tokens, timestep, mod_weight, qkv_weight, attn_scale, out_weight, grad_update):
-    embedded = embed(timestep, mod_weight.shape[0] // 2)
-    gain = 1.0 + jnp.sum(embedded[:, None] * mod_weight, 0)
-    tok_float = tokens.astype(jnp.float32)
-    rstd = lax.rsqrt(jnp.mean(tok_float * tok_float, -1, keepdims=True) + epsilon)
-    normed = tok_float * rstd
-    hidden = (normed * gain).astype(jnp.bfloat16)
-    update, grad_hidden, grad_qkv, grad_out = fused(
-        attn_scale, hidden, grad_update, qkv_weight, out_weight
+    length = tokens.shape[0] * lax.axis_size("row") * lax.axis_size("col")
+    if mod_weight.shape != (qkv_weight.shape[2], length):
+        return per_device(
+            tokens, timestep, mod_weight, qkv_weight, attn_scale, out_weight, grad_update
+        )
+    embedded = embed(timestep, mod_weight.shape[0] // 2)[:, None]
+    return tuple(
+        hand_over(
+            fused(attn_scale, embedded, tokens, grad_update, mod_weight, qkv_weight, out_weight)
+        )
     )
-    grad_normed = grad_hidden * gain
-    grad_tokens = (
-        rstd * (grad_normed - normed * jnp.mean(grad_normed * normed, -1, keepdims=True))
-    ).astype(jnp.bfloat16)
-    return (update.astype(jnp.bfloat16), grad_tokens, grad_qkv, grad_out)
 
 
 def solution(mesh):

time: 151 us -> 121 us (0.80); the launches traced: 151 us -> 119 us
  Pallas kernels: 139 us -> 116 us
  other arithmetic: 8.96 us -> 0.06 us
    pallas_call x1, Pallas kernels: 139 us -> 113 us  [fused(): pl.pallas_call(fused_kernel, out_shape=[jax.ShapeDtypeStruct((tok_dev, wi...]
    convert_element_type x3 -> x0, other arithmetic: 4.69 us -> none  [the longest x1 1.97 us: gathered(): grad_tokens = (rstd * (grad_normed - normed * jnp.mean(grad_normed * norm...]
    reduce_sum x3 -> x0, other arithmetic: 4.19 us -> none  [the longest x1 1.81 us: gathered(): gain = 1.0 + jnp.sum(embedded[:, None] * mod_weight, 0)]
    pallas_call x0 -> x1, Pallas kernels: none -> 2.96 us  [hand_over(): pl.pallas_call(hand_over_kernel, out_shape=[jax.ShapeDtypeStruct(a.shape,...]
    unnamed x8 -> x0, local copies, waits for them, and re-layouts: 1.95 us -> none
where the time goes in v3:
time: 121 us; the launch traced here: 119 us
  Pallas kernels  116 us (96%)
  between operations  1.46 us (1%)
    pallas_call x1, Pallas kernels, fused(): pl.pallas_call(fused_kernel, out_shape=[jax.ShapeDtypeStruct((tok_dev, wi...  113 us
    pallas_call x1, Pallas kernels, hand_over(): pl.pallas_call(hand_over_kernel, out_shape=[jax.ShapeDtypeStruct(a.shape,...  2.96 us

profile of v3, /device:TPU:0, one launch (start us, length us, event | category | flops | bytes accessed | tf_op | source)
XLA Modules:
  0.0 118.6 jit_solution(3584504554568327388)
XLA Ops:
  1.3 0.8 copy.11.embed_ref
  2.2 113.3 %fused.1 = (bf16[64,2048]{1,0:T(8,128)(2,1)}, bf16[64,2048]{1,0:T(8,128)(2,1)}, f32[3,512,256]{2,1,0:T(8,128)}, f32[256,512]{1,0:T(8,128)}) custom-call(f32[2]{0:T(128)} %scale_ref.1, f32[256,1]{1,0:T(8,128)} %copy.11.embed_ref, bf16[64,2048]{1,0:T(8,128)(2,1)} %tok_ref.1, bf16[64,2048]{1,0:T(8,128)(2,1)} %grad_ref.1, f32[256,2048]{1,0:T(8,128)} %mod_hbm.1, ...), custom_call_target="tpu_custom_call" | custom-call | tf_op jit(solution)/shard_map/fused/pallas_call | solution.py:984
  115.5 3.0 %hand_over.1 = (bf16[64,2048]{1,0:T(8,128)(2,1)}, bf16[64,2048]{1,0:T(8,128)(2,1)}, f32[3,512,256]{2,1,0:T(8,128)}, f32[256,512]{1,0:T(8,128)}) custom-call(bf16[64,2048]{1,0:T(8,128)(2,1)} %get-tuple-element.8.refs_0_, bf16[64,2048]{1,0:T(8,128)(2,1)} %get-tuple-element.9.refs_1_, f32[3,512,256]{2,1,0:T(8,128)} %get-tuple-element.10.refs_2_, ...), custom_call_target="tpu_custom_call" | custom-call | tf_op jit(solution)/shard_map/hand_over/pallas_call | solution.py:1054
  (2 shorter events, 0.1 us)

commit v4 on v3

--- a/solution.py
+++ b/solution.py
@@ -384,13 +384,32 @@
         pl.semaphore_wait(pltpu.get_barrier_semaphore(), 7)
 
 
-KINDS = 9
 LINE, BESIDE, ACROSS, TOP, BOTTOM, MATE = 0, 1, 2, 3, 4, 5
-SENDS = 12
+WHOLE, LEVEL, SLICE, BLOCK, FAR = 0, 1, 2, 3, 4
+LINES = (WHOLE, BLOCK, FAR)
+PLANES = [(WHOLE, rank) for rank in range(4)] + [(LEVEL, 0)] + [(SLICE, r) for r in (1, 2, 3)]
+
+
+def numbered(keys):
+    return {key: at for at, key in enumerate(keys)}
+
+
+SENDS = numbered(
+    [(job, rank, 0) for job in LINES for rank in range(4)]
+    + [(job, 0, 1) for job in LINES]
+    + [(SLICE, at, 0) for at in range(3)]
+    + [plane + (kind,) for plane in PLANES for kind in range(2, 10)]
+)
+ARRIVALS = numbered(
+    [(SLICE, row, LINE) for row in range(4)]
+    + [(job, rank, LINE) for job in LINES for rank in (1, 2, 3)]
+    + [plane + (kind,) for plane in PLANES for kind in range(1, 9)]
+)
 
 
 class Gather:
-    def __init__(self, place, job, tile, whole, send_sem, recv_sem):
+    def __init__(self, place, job, tile, whole, send_sem, recv_sem, split=False):
+        self.split = split
         self.place, self.job, self.tile, self.whole = place, job, tile, whole
         self.send_sem, self.recv_sem = send_sem, recv_sem
 
@@ -401,8 +420,8 @@
         return pltpu.make_async_remote_copy(
             src_ref=source,
             dst_ref=landing,
-            send_sem=self.send_sem.at[self.job, send[0], send[1]],
-            recv_sem=self.recv_sem.at[self.job, rank, kind],
+            send_sem=self.send_sem.at[SENDS.get((self.job,) + send, 0)],
+            recv_sem=self.recv_sem.at[ARRIVALS[self.job, rank, kind]],
             device_id=peer,
             device_id_type=MESH,
         )
@@ -434,13 +453,19 @@
             self.link(rank, MATE, (rank, 4), held, mine, {"col": p.partner}),
         ]
 
+    def strip(self, ref, rank, side):
+        if not self.split or rank == 0:
+            return half(ref, side)
+        size = ref.shape[0] // 4
+        return ref.at[pl.ds(side * size, size)]
+
     def relays(self, rank):
         p = self.place
         side, over = self.slot(rank, p.beside), self.slot(rank, p.across)
         return [
-            self.link(rank, TOP, (rank, 5), half(side, 0), half(side, 0), {"col": p.across}),
+            self.link(rank, TOP, (rank, 5), self.strip(side, rank, 0), self.strip(side, rank, 0), {"col": p.across}),
             self.link(rank, MATE + 1, (rank, 6), side, side, {"col": p.partner}),
-            self.link(rank, BOTTOM, (rank, 7), half(over, 1), half(over, 1), {"col": p.beside}),
+            self.link(rank, BOTTOM, (rank, 7), self.strip(over, rank, 1), self.strip(over, rank, 1), {"col": p.beside}),
             self.link(rank, MATE + 2, (rank, 8), over, over, {"col": p.partner}),
         ]
 
@@ -477,8 +502,8 @@
     def close(self, rank):
         p = self.place
         far = self.slot(rank, p.corner)
-        self.arrived(rank, TOP, half(far, 0))
-        self.arrived(rank, BOTTOM, half(far, 1))
+        self.arrived(rank, TOP, self.strip(far, rank, 0))
+        self.arrived(rank, BOTTOM, self.strip(far, rank, 1))
         self.last(rank).start()
 
     def whole_rank(self, rank):
@@ -503,6 +528,11 @@
 class Line(Gather):
     def slot(self, rank, col):
         return self.whole.at[self.place.ranks[rank]]
+
+
+class Corner(Gather):
+    def slot(self, rank, col):
+        return half(self.whole.at[self.place.ranks[rank], self.place.corner], 1)
 
 
 class Slices(Gather):
@@ -516,8 +546,8 @@
                 pltpu.make_async_remote_copy(
                     src_ref=self.tile.at[:, mine],
                     dst_ref=self.slot(0, p.col),
-                    send_sem=self.send_sem.at[self.job, at, 0],
-                    recv_sem=self.recv_sem.at[self.job, p.row, LINE],
+                    send_sem=self.send_sem.at[SENDS[self.job, at, 0]],
+                    recv_sem=self.recv_sem.at[p.row],
                     device_id={"row": peer},
                     device_id_type=MESH,
                 )
@@ -530,8 +560,8 @@
         pltpu.make_async_remote_copy(
             src_ref=slot,
             dst_ref=slot,
-            send_sem=self.send_sem.at[self.job, 0, 0],
-            recv_sem=self.recv_sem.at[self.job, p.ranks[rank], LINE],
+            send_sem=self.send_sem.at[SENDS[self.job, 0, 0]],
+            recv_sem=self.recv_sem.at[p.ranks[rank]],
             device_id={"col": p.partner},
             device_id_type=MESH,
         ).wait_recv()
@@ -611,8 +641,8 @@
 
 def fused_kernel(
     scale_ref, embed_ref, tok_ref, grad_ref, mod_hbm, qkv_hbm, out_hbm,
-    update_ref, grad_tok_ref, grad_qkv_ref, grad_out_ref,
-    hidden_ref, gain_ref, qkv_ref, out_ref, load_sem, hid_all, grad_level, grad_cut, do_all, raw_ref, q_ref, qt_ref, k_ref, kt_ref, v_ref, vt_ref,
+    update_hbm, grad_tok_hbm, grad_qkv_hbm, grad_out_hbm,
+    update_ref, grad_tok_ref, grad_qkv_ref, grad_out_ref, hidden_ref, gain_ref, qkv_ref, out_ref, load_sem, hid_all, grad_level, grad_cut, do_all, raw_ref, q_ref, qt_ref, k_ref, kt_ref, v_ref, vt_ref,
     w_ref, inv_ref, own_ref, att_ref, dot_ref, dkt_ref, dvt_ref, gr_ref,
     part_ref, crossed, landed, send_sem, recv_sem, send_sum, recv_sum,
 ):
@@ -635,6 +665,17 @@
         pltpu.make_async_copy(qkv_hbm, qkv_ref, load_sem.at[0]),
         pltpu.make_async_copy(out_hbm, out_ref, load_sem.at[1]),
     ]
+    stores = [
+        pltpu.make_async_copy(held, to, load_sem.at[2 + heads + at])
+        for at, (held, to) in enumerate(
+            (
+                (update_ref, update_hbm),
+                (grad_tok_ref, grad_tok_hbm),
+                (grad_qkv_ref, grad_qkv_hbm),
+                (grad_out_ref, grad_out_hbm),
+            )
+        )
+    ]
     for load in mod_loads + loads:
         load.start()
     place.greet()
@@ -652,7 +693,10 @@
 
     hidden_ref[...] = (normed_rows()[0] * gain_ref[0:1, :]).astype(bf)
     place.await_greetings()
-    hid = Gather(place, 0, hidden_ref, hid_all, send_sem, recv_sem)
+    hid = Gather(place, 0, hidden_ref, hid_all, send_sem, recv_sem, True)
+    far = Corner(
+        place, 4, half(hid_all.at[place.row, place.corner], 1), hid_all, send_sem, recv_sem
+    )
     grd = Level(place, 1, grad_ref, grad_level, send_sem, recv_sem)
     cut = Slices(place, 2, grad_ref, grad_cut, send_sem, recv_sem)
     dol = Line(place, 3, do_all.at[place.row], do_all, send_sem, recv_sem)
@@ -871,6 +915,7 @@
 
     hid.relay(1)
     hid.close(0)
+    start_all(far.line_sends(0))
     hid.whole_rank(0)
     for load in loads:
         load.wait()
@@ -883,15 +928,36 @@
     hid.spread(3)
     for copy in cut.cuts():
         copy.start()
+    far.pass_on(1)
     hid.relay(2)
     hid.close(1)
+
+    @pl.when(place.inner)
+    def _():
+        far.pass_on(2)
+
     hid.whole_rank(1)
     project(1)
+
+    @pl.when(place.inner)
+    def _():
+        far.pass_on(3)
+
     hid.relay(3)
     grd.spread(0)
+
+    @pl.when(jnp.logical_not(place.inner))
+    def _():
+        far.arrived(2, LINE, far.slot(2, place.col))
+
     hid.close(2)
     hid.whole_rank(2)
     project(2)
+
+    @pl.when(jnp.logical_not(place.inner))
+    def _():
+        far.arrived(3, LINE, far.slot(3, place.col))
+
     hid.close(3)
     hid.whole_rank(3)
     project(3)
@@ -917,12 +983,12 @@
 
     forward(3)
     prepare(0)
+    backward(0, (0, 1, 2, 3))
 
     @pl.when(place.inner)
     def _():
         dol.pass_on(3)
 
-    backward(0, (0, 1, 2, 3))
     cut.relay(1)
     cut.relay(2)
     prepare(1)
@@ -946,20 +1012,25 @@
     prepare(3)
     backward(3, (0,))
     update_ref[...] = scatters[0].third().astype(update_ref.dtype)
+    stores[0].start()
     finish_keys(0)
     project_down()
     scatters[1].first()
     for rank in range(1, 4):
         cut.whole_rank(rank)
     out_grads()
+    stores[3].start()
     scatters[1].second()
     backward(2, (1, 2, 3), (0,))
     backward(3, (1, 2, 3), (0,))
     for rank in range(1, 4):
         finish_keys(rank)
     weight_grads()
+    stores[2].start()
     tokens_grad(scatters[1].third())
+    stores[1].start()
     hid.drain_line()
+    far.drain_line()
     dol.drain_line()
     grd.drain_plane(0)
     for copy in cut.cuts():
@@ -968,6 +1039,8 @@
         hid.drain_plane(rank)
         if rank > 0:
             cut.drain_plane(rank)
+    for store in stores:
+        store.wait()
 
 
 def fused(scale, embedded, tokens, grad_update, mod_weight, qkv_weight, out_weight):
@@ -992,13 +1065,17 @@
         in_specs=[pl.BlockSpec(memory_space=pltpu.SMEM)]
         + [in_vmem] * 3
         + [pl.BlockSpec(memory_space=pl.ANY)] * 3,
-        out_specs=[in_vmem] * 4,
+        out_specs=[pl.BlockSpec(memory_space=pl.ANY)] * 4,
         scratch_shapes=[
+            pltpu.VMEM((tok_dev, width), bf),
+            pltpu.VMEM((tok_dev, width), bf),
+            pltpu.VMEM((3, narrow, inner), f32),
+            pltpu.VMEM((inner, narrow), f32),
             pltpu.VMEM((tok_dev, width), bf),
             pltpu.VMEM((8, width), f32),
             pltpu.VMEM(qkv_weight.shape, bf),
             pltpu.VMEM(out_weight.shape, bf),
-            pltpu.SemaphoreType.DMA((2 + heads,)),
+            pltpu.SemaphoreType.DMA((6 + heads,)),
             pltpu.VMEM((rows, cols, tok_dev, width), bf),
             pltpu.VMEM((cols, tok_dev, width), bf),
             pltpu.VMEM((rows, cols, tok_dev, narrow), bf),
@@ -1021,8 +1098,8 @@
             pltpu.VMEM((span, width), bf),
             pltpu.VMEM((2, 4, tok_dev, width), bf),
             pltpu.VMEM((2, 3, tok_dev, width), bf),
-            pltpu.SemaphoreType.DMA((4, 4, SENDS)),
-            pltpu.SemaphoreType.DMA((4, 4, KINDS)),
+            pltpu.SemaphoreType.DMA((len(SENDS),)),
+            pltpu.SemaphoreType.DMA((len(ARRIVALS),)),
             pltpu.SemaphoreType.DMA((2, 8)),
             pltpu.SemaphoreType.DMA((2, 8)),
         ],

time: 121 us -> 115 us (0.950); the launches traced: 119 us -> 115 us
  Pallas kernels: 116 us -> 113 us
    pallas_call x1, Pallas kernels: 113 us -> 110 us  [fused(): pl.pallas_call(fused_kernel, out_shape=[jax.ShapeDtypeStruct((tok_dev, wi...]
where the time goes in v4:
time: 115 us
  Pallas kernels  113 us (98%)
  between operations  1.46 us (1%)
    pallas_call x1, Pallas kernels, fused(): pl.pallas_call(fused_kernel, out_shape=[jax.ShapeDtypeStruct((tok_dev, wi...  110 us
    pallas_call x1, Pallas kernels, hand_over(): pl.pallas_call(hand_over_kernel, out_shape=[jax.ShapeDtypeStruct(a.shape,...  2.96 us

profile of v4, /device:TPU:0, one launch (start us, length us, event | category | flops | bytes accessed | tf_op | source)
XLA Modules:
  0.0 115.3 jit_solution(737796675185833800)
XLA Ops:
  1.3 0.8 copy.11.embed_ref
  2.2 110.0 %fused.1 = (bf16[64,2048]{1,0:T(8,128)(2,1)}, bf16[64,2048]{1,0:T(8,128)(2,1)}, f32[3,512,256]{2,1,0:T(8,128)}, f32[256,512]{1,0:T(8,128)}) custom-call(f32[2]{0:T(128)} %scale_ref.1, f32[256,1]{1,0:T(8,128)} %copy.11.embed_ref, bf16[64,2048]{1,0:T(8,128)(2,1)} %tok_ref.1, bf16[64,2048]{1,0:T(8,128)(2,1)} %grad_ref.1, f32[256,2048]{1,0:T(8,128)} %mod_hbm.1, ...), custom_call_target="tpu_custom_call" | custom-call | tf_op jit(solution)/shard_map/fused/pallas_call | solution.py:1057
  112.2 3.0 %hand_over.1 = (bf16[64,2048]{1,0:T(8,128)(2,1)}, bf16[64,2048]{1,0:T(8,128)(2,1)}, f32[3,512,256]{2,1,0:T(8,128)}, f32[256,512]{1,0:T(8,128)}) custom-call(bf16[64,2048]{1,0:T(8,128)(2,1)} %get-tuple-element.8.refs_0_, bf16[64,2048]{1,0:T(8,128)(2,1)} %get-tuple-element.9.refs_1_, f32[3,512,256]{2,1,0:T(8,128)} %get-tuple-element.10.refs_2_, ...), custom_call_target="tpu_custom_call" | custom-call | tf_op jit(solution)/shard_map/hand_over/pallas_call | solution.py:1131
  (2 shorter events, 0.1 us)

commit v5 on v4

--- a/solution.py
+++ b/solution.py
@@ -682,7 +682,8 @@
     gain = 1.0
     for head, load in enumerate(mod_loads):
         load.wait()
-        here = embed_ref[pl.ds(head * hdim, hdim), :] * dkt_ref[head]
+        waves = jnp.broadcast_to(embed_ref[head : head + 1, :], (hdim, hdim)).T[:, :1]
+        here = waves * dkt_ref[head]
         gain = gain + jnp.sum(here, 0, keepdims=True)
     gain_ref[...] = jnp.broadcast_to(gain, gain_ref.shape)
 
@@ -759,18 +760,34 @@
 
     wide = min(512, span)
 
-    def forward(rank):
+    def key_spans(key_rank):
+        first = pl.multiple_of(place.ranks[key_rank] * span, span)
+        for start in range(0, span, wide):
+            yield pl.ds(pl.multiple_of(first + start, wide), wide)
+
+    def weigh(head, at, here):
+        coeff = scale_ref[head] * (LOG2E / hdim)
+        weights = jnp.exp2(dot(q_ref[head, at, :], kt_ref[head, :, here]) * coeff).astype(bf)
+        w_ref[head, at, here] = weights
+        return weights
+
+    def weigh_early(pairs):
+        def body(head, chunk):
+            for rank, key_rank in pairs:
+                for here in key_spans(key_rank):
+                    weigh(head, pl.ds(tokens_at(rank, chunk), size), here)
+
+        blocks(body)
+
+    def forward(rank, weighed=()):
         def body(head, chunk):
             at = pl.ds(tokens_at(rank, chunk), size)
-            coeff = scale_ref[head] * (LOG2E / hdim)
-            query = q_ref[head, at, :]
             mixed = None
-            for start in range(0, length, wide):
-                here = pl.ds(start, wide)
-                weights = jnp.exp2(dot(query, kt_ref[head, :, here]) * coeff).astype(bf)
-                w_ref[head, at, here] = weights
-                more = dot(weights, v_ref[head, here, :])
-                mixed = more if mixed is None else mixed + more
+            for key_rank in range(rows):
+                for here in key_spans(key_rank):
+                    weights = w_ref[head, at, here] if key_rank in weighed else weigh(head, at, here)
+                    more = dot(weights, v_ref[head, here, :])
+                    mixed = more if mixed is None else mixed + more
             inverse = 1.0 / mixed[:, hdim:]
             attended = (mixed[:, :hdim] * inverse).astype(bf)
             if rank == 0:
@@ -945,6 +962,7 @@
 
     hid.relay(3)
     grd.spread(0)
+    weigh_early([(0, 0), (0, 1), (1, 0), (1, 1)])
 
     @pl.when(jnp.logical_not(place.inner))
     def _():
@@ -953,6 +971,7 @@
     hid.close(2)
     hid.whole_rank(2)
     project(2)
+    weigh_early([(0, 2), (1, 2), (2, 0), (2, 1), (2, 2)])
 
     @pl.when(jnp.logical_not(place.inner))
     def _():
@@ -962,7 +981,7 @@
     hid.whole_rank(3)
     project(3)
     grd.relay(0)
-    forward(0)
+    forward(0, (0, 1, 2))
     grd.close(0)
     project_out()
     scatters[0].first()
@@ -973,8 +992,8 @@
     for rank in range(1, 4):
         cut.landed(rank)
         cut.spread(rank)
-    forward(1)
-    forward(2)
+    forward(1, (0, 1, 2))
+    forward(2, (0, 1, 2))
     dol.pass_on(1)
 
     @pl.when(place.inner)
@@ -1145,7 +1164,7 @@
         return per_device(
             tokens, timestep, mod_weight, qkv_weight, attn_scale, out_weight, grad_update
         )
-    embedded = embed(timestep, mod_weight.shape[0] // 2)[:, None]
+    embedded = embed(timestep, mod_weight.shape[0] // 2).reshape(attn_scale.shape[0], -1)
     return tuple(
         hand_over(
             fused(attn_scale, embedded, tokens, grad_update, mod_weight, qkv_weight, out_weight)

time: 115 us -> 117 us (1.017)
  Pallas kernels: 113 us -> 115 us
    pallas_call x1, Pallas kernels: 110 us -> 112 us  [fused(): pl.pallas_call(fused_kernel, out_shape=[jax.ShapeDtypeStruct((tok_dev, wi...]
where the time goes in v5:
time: 117 us
  Pallas kernels  115 us (98%)
  between operations  1.45 us (1%)
    pallas_call x1, Pallas kernels, fused(): pl.pallas_call(fused_kernel, out_shape=[jax.ShapeDtypeStruct((tok_dev, wi...  112 us
    pallas_call x1, Pallas kernels, hand_over(): pl.pallas_call(hand_over_kernel, out_shape=[jax.ShapeDtypeStruct(a.shape,...  2.96 us

profile of v5, /device:TPU:0, one launch (start us, length us, event | category | flops | bytes accessed | tf_op | source)
XLA Modules:
  0.0 116.6 jit_solution(8184533335612581616)
XLA Ops:
  1.3 0.6 maximum_bitcast_fusion.embed_ref
  1.9 111.6 %fused.1 = (bf16[64,2048]{1,0:T(8,128)(2,1)}, bf16[64,2048]{1,0:T(8,128)(2,1)}, f32[3,512,256]{2,1,0:T(8,128)}, f32[256,512]{1,0:T(8,128)}) custom-call(f32[2]{0:T(128)} %scale_ref.1, f32[2,128]{1,0:T(2,128)} %maximum_bitcast_fusion.embed_ref, bf16[64,2048]{1,0:T(8,128)(2,1)} %tok_ref.1, bf16[64,2048]{1,0:T(8,128)(2,1)} %grad_ref.1, f32[256,2048]{1,0:T(8,128)} %mod_hbm.1, ...), custom_call_target="tpu_custom_call" | custom-call | tf_op jit(solution)/shard_map/fused/pallas_call | solution.py:1076
  113.5 3.0 %hand_over.1 = (bf16[64,2048]{1,0:T(8,128)(2,1)}, bf16[64,2048]{1,0:T(8,128)(2,1)}, f32[3,512,256]{2,1,0:T(8,128)}, f32[256,512]{1,0:T(8,128)}) custom-call(bf16[64,2048]{1,0:T(8,128)(2,1)} %get-tuple-element.8.refs_0_, bf16[64,2048]{1,0:T(8,128)(2,1)} %get-tuple-element.9.refs_1_, f32[3,512,256]{2,1,0:T(8,128)} %get-tuple-element.10.refs_2_, ...), custom_call_target="tpu_custom_call" | custom-call | tf_op jit(solution)/shard_map/hand_over/pallas_call | solution.py:1150
  (1 shorter events, 0.0 us)
